TPU v7x, 32 devices: a whole 2x2x4 slice. The times are simulated.
32 devices in a mesh: rep: 4 (over z), fsdp: 8 (over y, x, core).
Axes of the slice: x: 2, y: 2, z: 4, core: 2. Of those that a mesh axis runs over, the one named last changes fastest.
Arguments:
- hidden_in: float32 [32768, 384], P(('rep', 'fsdp')), may hold values from -6 to 6
- cotangent: float32 [32768, 384], P(('rep', 'fsdp')), may hold values from -6 to 6
- segment_ids: int32 [32768], P(('rep', 'fsdp')), may hold values from -1 to 4, as said below
- norm1_gain: bfloat16 [2, 384], P(None, 'fsdp'), may hold values from 0.5 to 1.5
- norm1_bias: bfloat16 [2, 384], P(None, 'fsdp'), may hold values from -3 to 3
- qkv_weight: bfloat16 [2, 384, 1152], P(None, 'fsdp'), may hold values from -0.3125 to 0.3125
- query_bias: bfloat16 [2, 384], P(None, 'fsdp'), may hold values from -3 to 3
- value_bias: bfloat16 [2, 384], P(None, 'fsdp'), may hold values from -3 to 3
- out_weight: bfloat16 [2, 384, 384], P(None, 'fsdp'), may hold values from -1.25 to 1.25
- out_bias: bfloat16 [2, 384], P(None, 'fsdp'), may hold values from -3 to 3
- norm2_gain: bfloat16 [2, 384], P(None, 'fsdp'), may hold values from 0.5 to 1.5
- norm2_bias: bfloat16 [2, 384], P(None, 'fsdp'), may hold values from -3 to 3
- up_weight: bfloat16 [2, 384, 1536], P(None, 'fsdp'), may hold values from -0.3125 to 0.3125
- up_bias: bfloat16 [2, 1536], P(None, 'fsdp'), may hold values from -3 to 3
- down_weight: bfloat16 [2, 1536, 384], P(None, 'fsdp'), may hold values from -0.15625 to 0.15625
- down_bias: bfloat16 [2, 384], P(None, 'fsdp'), may hold values from -3 to 3
Outputs:
- output: float32 [32768, 384], P(('rep', 'fsdp'))
- grad_input: float32 [32768, 384], P(('rep', 'fsdp'))
- grad_norm1_gain: float32 [2, 384], P(None, 'fsdp')
- grad_norm1_bias: float32 [2, 384], P(None, 'fsdp')
- grad_qkv_weight: float32 [2, 384, 1152], P(None, 'fsdp')
- grad_query_bias: float32 [2, 384], P(None, 'fsdp')
- grad_value_bias: float32 [2, 384], P(None, 'fsdp')
- grad_out_weight: float32 [2, 384, 384], P(None, 'fsdp')
- grad_out_bias: float32 [2, 384], P(None, 'fsdp')
- grad_norm2_gain: float32 [2, 384], P(None, 'fsdp')
- grad_norm2_bias: float32 [2, 384], P(None, 'fsdp')
- grad_up_weight: float32 [2, 384, 1536], P(None, 'fsdp')
- grad_up_bias: float32 [2, 1536], P(None, 'fsdp')
- grad_down_weight: float32 [2, 1536, 384], P(None, 'fsdp')
- grad_down_bias: float32 [2, 384], P(None, 'fsdp')
Inputs may be any that keep to these rules, and one draw needn't show every extreme that they name: `segment_ids`: in each aligned block of 1024 slots, images of 197 tokens are numbered 0, 1, 2 ... from the block's start, each whole and contiguous, followed by -1 in all remaining slots; a block holds 2 to 5 images, and some block holds 5.
All inputs are finite; a program needn't handle non-finite values.
Results may differ from a plain program's by a relative error of at most 0.012.
Values may be sent and summed in bfloat16 or wider, within the bound.
A program may use at most 256 MiB of HBM per device.

v0:
```python
import jax
import jax.numpy as jnp
from jax import lax
from jax.sharding import PartitionSpec as P

HEADS = 6
HEAD_DIM = 64


norm_eps = 1e-06
neg_fill = -1e30
root_half = 0.7071067811865476
inv_root_tau = 0.3989422804014327


def norm_forward(stream, gain_vec, bias_vec):
    center = stream - jnp.mean(stream, -1, keepdims=True)
    recip = lax.rsqrt(jnp.mean(center * center, -1, keepdims=True) + norm_eps)
    normed = center * recip
    return (normed * gain_vec.astype(jnp.float32) + bias_vec.astype(jnp.float32), normed, recip)


def norm_backward(grad_norm, normed, recip, gain_vec):
    scaled = grad_norm * gain_vec.astype(jnp.float32)
    grad_stream = recip * (
        scaled
        - jnp.mean(scaled, -1, keepdims=True)
        - normed * jnp.mean(scaled * normed, -1, keepdims=True)
    )
    return (grad_stream, jnp.sum(grad_norm * normed, 0), jnp.sum(grad_norm, 0))


def gelu_value(pre_act):
    return 0.5 * pre_act * (1.0 + lax.erf(pre_act * root_half))


def gelu_slope(pre_act):
    return (
        0.5 * (1.0 + lax.erf(pre_act * root_half))
        + pre_act * jnp.exp(-0.5 * pre_act * pre_act) * inv_root_tau
    )


def matmul(left, right):
    return jnp.dot(left, right, preferred_element_type=jnp.float32)


def split_heads(rows_arr):
    return rows_arr.reshape(rows_arr.shape[0], HEADS, HEAD_DIM)


def masked_scores(query_blk, key_all, seg_blk, seg_all):
    scores = jnp.einsum("qhd,khd->hqk", query_blk, key_all, preferred_element_type=jnp.float32)
    same_image = seg_blk[:, None] == seg_all[None, :]
    return jnp.where(same_image[None], scores, neg_fill)


def attend_forward(query_all, key_all, value_all, seg_all):
    count = query_all.shape[0]
    block = min(512, count)
    query3 = split_heads(query_all)
    key3 = split_heads(key_all)
    value3 = split_heads(value_all)
    pieces = []
    totals = []
    for start in range(0, count, block):
        scores = masked_scores(
            query3[start : start + block], key3, seg_all[start : start + block], seg_all
        )
        top_score = jnp.max(scores, -1, keepdims=True)
        expo = jnp.exp(scores - top_score)
        denom = jnp.sum(expo, -1, keepdims=True)
        probs_low = (expo / denom).astype(jnp.bfloat16)
        mixed = jnp.einsum("hqk,khd->qhd", probs_low, value3, preferred_element_type=jnp.float32)
        pieces.append(mixed.reshape(block, -1).astype(jnp.bfloat16))
        totals.append((top_score + jnp.log(denom))[:, :, 0])
    return (jnp.concatenate(pieces, 0), jnp.concatenate(totals, 1))


def attend_backward(query_all, key_all, value_all, seg_all, log_total, grad_mixed):
    count = query_all.shape[0]
    block = min(512, count)
    query3 = split_heads(query_all)
    key3 = split_heads(key_all)
    value3 = split_heads(value_all)
    grad3 = split_heads(grad_mixed)
    grad_key = jnp.zeros((count, HEADS, HEAD_DIM), jnp.float32)
    grad_value = jnp.zeros((count, HEADS, HEAD_DIM), jnp.float32)
    grad_query = []
    for start in range(0, count, block):
        scores = masked_scores(
            query3[start : start + block], key3, seg_all[start : start + block], seg_all
        )
        probs = jnp.exp(scores - log_total[:, start : start + block, None])
        probs_low = probs.astype(jnp.bfloat16)
        grad_blk = grad3[start : start + block]
        grad_probs = jnp.einsum(
            "qhd,khd->hqk", grad_blk, value3, preferred_element_type=jnp.float32
        )
        delta = jnp.sum(probs * grad_probs, -1, keepdims=True)
        grad_scores = (probs * (grad_probs - delta)).astype(jnp.bfloat16)
        grad_query.append(
            jnp.einsum(
                "hqk,khd->qhd", grad_scores, key3, preferred_element_type=jnp.float32
            ).reshape(block, -1)
        )
        grad_key = grad_key + jnp.einsum(
            "hqk,qhd->khd",
            grad_scores,
            query3[start : start + block],
            preferred_element_type=jnp.float32,
        )
        grad_value = grad_value + jnp.einsum(
            "hqk,qhd->khd", probs_low, grad_blk, preferred_element_type=jnp.float32
        )
    return (
        jnp.concatenate(grad_query, 0),
        grad_key.reshape(count, -1),
        grad_value.reshape(count, -1),
    )


def layer_forward(stream, seg_all, params):
    (
        norm1_gain,
        norm1_bias,
        qkv_weight,
        query_bias,
        value_bias,
        out_weight,
        out_bias,
        norm2_gain,
        norm2_bias,
        up_weight,
        up_bias,
        down_weight,
        down_bias,
    ) = params
    width = stream.shape[1]
    scale = HEAD_DIM ** (-0.5)
    normed_a = norm_forward(stream, norm1_gain, norm1_bias)[0].astype(jnp.bfloat16)
    proj = matmul(normed_a, qkv_weight)
    query = ((proj[:, :width] + query_bias.astype(jnp.float32)) * scale).astype(jnp.bfloat16)
    key_rows = proj[:, width : 2 * width].astype(jnp.bfloat16)
    value_rows = (proj[:, 2 * width :] + value_bias.astype(jnp.float32)).astype(jnp.bfloat16)
    attended, log_total = attend_forward(query, key_rows, value_rows, seg_all)
    stream_mid = stream + matmul(attended, out_weight) + out_bias.astype(jnp.float32)
    normed_m = norm_forward(stream_mid, norm2_gain, norm2_bias)[0].astype(jnp.bfloat16)
    pre_act = matmul(normed_m, up_weight) + up_bias.astype(jnp.float32)
    hidden = gelu_value(pre_act).astype(jnp.bfloat16)
    stream_out = stream_mid + matmul(hidden, down_weight) + down_bias.astype(jnp.float32)
    return (
        stream_out,
        (
            stream,
            normed_a,
            query,
            key_rows,
            value_rows,
            attended,
            log_total,
            stream_mid,
            normed_m,
            pre_act,
            hidden,
        ),
    )


def layer_backward(grad_out, seg_all, params, saved):
    (
        norm1_gain,
        norm1_bias,
        qkv_weight,
        query_bias,
        value_bias,
        out_weight,
        out_bias,
        norm2_gain,
        norm2_bias,
        up_weight,
        up_bias,
        down_weight,
        down_bias,
    ) = params
    (
        stream,
        normed_a,
        query,
        key_rows,
        value_rows,
        attended,
        log_total,
        stream_mid,
        normed_m,
        pre_act,
        hidden,
    ) = saved
    scale = HEAD_DIM ** (-0.5)
    grad_out_low = grad_out.astype(jnp.bfloat16)
    grad_down_bias = jnp.sum(grad_out, 0)
    grad_down_weight = matmul(hidden.T, grad_out_low)
    grad_pre = matmul(grad_out_low, down_weight.T) * gelu_slope(pre_act)
    grad_pre_low = grad_pre.astype(jnp.bfloat16)
    grad_up_bias = jnp.sum(grad_pre, 0)
    grad_up_weight = matmul(normed_m.T, grad_pre_low)
    grad_m = matmul(grad_pre_low, up_weight.T)
    unused2, normed2, recip2 = norm_forward(stream_mid, norm2_gain, norm2_bias)
    grad_stream2, grad_norm2_gain, grad_norm2_bias = norm_backward(
        grad_m, normed2, recip2, norm2_gain
    )
    grad_mid = grad_out + grad_stream2
    grad_mid_low = grad_mid.astype(jnp.bfloat16)
    grad_out_bias = jnp.sum(grad_mid, 0)
    grad_out_weight = matmul(attended.T, grad_mid_low)
    grad_attended = matmul(grad_mid_low, out_weight.T).astype(jnp.bfloat16)
    grad_query, grad_key, grad_value = attend_backward(
        query, key_rows, value_rows, seg_all, log_total, grad_attended
    )
    grad_query = grad_query * scale
    grad_proj = jnp.concatenate([grad_query, grad_key, grad_value], 1).astype(jnp.bfloat16)
    grad_query_bias = jnp.sum(grad_query, 0)
    grad_value_bias = jnp.sum(grad_value, 0)
    grad_qkv_weight = matmul(normed_a.T, grad_proj)
    grad_a = matmul(grad_proj, qkv_weight.T)
    unused1, normed1, recip1 = norm_forward(stream, norm1_gain, norm1_bias)
    grad_stream1, grad_norm1_gain, grad_norm1_bias = norm_backward(
        grad_a, normed1, recip1, norm1_gain
    )
    grads = (
        grad_norm1_gain,
        grad_norm1_bias,
        grad_qkv_weight,
        grad_query_bias,
        grad_value_bias,
        grad_out_weight,
        grad_out_bias,
        grad_norm2_gain,
        grad_norm2_bias,
        grad_up_weight,
        grad_up_bias,
        grad_down_weight,
        grad_down_bias,
    )
    return (grad_mid + grad_stream1, grads)


def fetch_forward(shards, layer_idx):
    return (
        lax.all_gather(shards[0][layer_idx], "fsdp", axis=0, tiled=True),
        lax.all_gather(shards[1][layer_idx], "fsdp", axis=0, tiled=True),
        lax.all_gather(shards[2][layer_idx], "fsdp", axis=0, tiled=True),
        lax.all_gather(shards[3][layer_idx], "fsdp", axis=0, tiled=True),
        lax.all_gather(shards[4][layer_idx], "fsdp", axis=0, tiled=True),
        lax.all_gather(shards[5][layer_idx], "fsdp", axis=0, tiled=True),
        lax.all_gather(shards[6][layer_idx], "fsdp", axis=0, tiled=True),
        lax.all_gather(shards[7][layer_idx], "fsdp", axis=0, tiled=True),
        lax.all_gather(shards[8][layer_idx], "fsdp", axis=0, tiled=True),
        lax.all_gather(shards[9][layer_idx], "fsdp", axis=0, tiled=True),
        lax.all_gather(shards[10][layer_idx], "fsdp", axis=0, tiled=True),
        lax.all_gather(shards[11][layer_idx], "fsdp", axis=0, tiled=True),
        lax.all_gather(shards[12][layer_idx], "fsdp", axis=0, tiled=True),
    )


def fetch_backward(shards, layer_idx):
    return (
        lax.all_gather(shards[0][layer_idx], "fsdp", axis=0, tiled=True),
        lax.all_gather(shards[1][layer_idx], "fsdp", axis=0, tiled=True),
        lax.all_gather(shards[2][layer_idx], "fsdp", axis=0, tiled=True),
        lax.all_gather(shards[3][layer_idx], "fsdp", axis=0, tiled=True),
        lax.all_gather(shards[4][layer_idx], "fsdp", axis=0, tiled=True),
        lax.all_gather(shards[5][layer_idx], "fsdp", axis=0, tiled=True),
        lax.all_gather(shards[6][layer_idx], "fsdp", axis=0, tiled=True),
        lax.all_gather(shards[7][layer_idx], "fsdp", axis=0, tiled=True),
        lax.all_gather(shards[8][layer_idx], "fsdp", axis=0, tiled=True),
        lax.all_gather(shards[9][layer_idx], "fsdp", axis=0, tiled=True),
        lax.all_gather(shards[10][layer_idx], "fsdp", axis=0, tiled=True),
        lax.all_gather(shards[11][layer_idx], "fsdp", axis=0, tiled=True),
        lax.all_gather(shards[12][layer_idx], "fsdp", axis=0, tiled=True),
    )


def local(
    hidden_in,
    cotangent,
    segment_ids,
    norm1_gain,
    norm1_bias,
    qkv_weight,
    query_bias,
    value_bias,
    out_weight,
    out_bias,
    norm2_gain,
    norm2_bias,
    up_weight,
    up_bias,
    down_weight,
    down_bias,
):
    shards = (
        norm1_gain,
        norm1_bias,
        qkv_weight,
        query_bias,
        value_bias,
        out_weight,
        out_bias,
        norm2_gain,
        norm2_bias,
        up_weight,
        up_bias,
        down_weight,
        down_bias,
    )
    layer_count = norm1_gain.shape[0]
    totals = [None] * layer_count
    stream = hidden_in
    saves = []
    for layer_idx in range(layer_count):
        layer_params = fetch_forward(shards, layer_idx)
        stream, saved = layer_forward(stream, segment_ids, layer_params)
        saves.append(saved)
    grad_now = cotangent * (segment_ids >= 0).astype(jnp.float32)[:, None]
    for layer_idx in range(layer_count - 1, -1, -1):
        layer_params = fetch_backward(shards, layer_idx)
        grad_now, grads = layer_backward(grad_now, segment_ids, layer_params, saves[layer_idx])
        totals[layer_idx] = grads
    stacked = tuple(
        (
            jnp.stack([totals[layer_idx][field] for layer_idx in range(layer_count)], 0)
            for field in range(13)
        )
    )
    shard_sums = (
        lax.psum_scatter(stacked[0], "fsdp", scatter_dimension=1, tiled=True),
        lax.psum_scatter(stacked[1], "fsdp", scatter_dimension=1, tiled=True),
        lax.psum_scatter(stacked[2], "fsdp", scatter_dimension=1, tiled=True),
        lax.psum_scatter(stacked[3], "fsdp", scatter_dimension=1, tiled=True),
        lax.psum_scatter(stacked[4], "fsdp", scatter_dimension=1, tiled=True),
        lax.psum_scatter(stacked[5], "fsdp", scatter_dimension=1, tiled=True),
        lax.psum_scatter(stacked[6], "fsdp", scatter_dimension=1, tiled=True),
        lax.psum_scatter(stacked[7], "fsdp", scatter_dimension=1, tiled=True),
        lax.psum_scatter(stacked[8], "fsdp", scatter_dimension=1, tiled=True),
        lax.psum_scatter(stacked[9], "fsdp", scatter_dimension=1, tiled=True),
        lax.psum_scatter(stacked[10], "fsdp", scatter_dimension=1, tiled=True),
        lax.psum_scatter(stacked[11], "fsdp", scatter_dimension=1, tiled=True),
        lax.psum_scatter(stacked[12], "fsdp", scatter_dimension=1, tiled=True),
    )
    summed = lax.psum(
        (
            shard_sums[0],
            shard_sums[1],
            shard_sums[2],
            shard_sums[3],
            shard_sums[4],
            shard_sums[5],
            shard_sums[6],
            shard_sums[7],
            shard_sums[8],
            shard_sums[9],
            shard_sums[10],
            shard_sums[11],
            shard_sums[12],
        ),
        "rep",
    )
    return (
        stream,
        grad_now,
        summed[0],
        summed[1],
        summed[2],
        summed[3],
        summed[4],
        summed[5],
        summed[6],
        summed[7],
        summed[8],
        summed[9],
        summed[10],
        summed[11],
        summed[12],
    )


def solution(mesh):
    in_specs = (
        P(("rep", "fsdp"), None),
        P(("rep", "fsdp"), None),
        P(("rep", "fsdp")),
        P(None, "fsdp"),
        P(None, "fsdp"),
        P(None, "fsdp", None),
        P(None, "fsdp"),
        P(None, "fsdp"),
        P(None, "fsdp", None),
        P(None, "fsdp"),
        P(None, "fsdp"),
        P(None, "fsdp"),
        P(None, "fsdp", None),
        P(None, "fsdp"),
        P(None, "fsdp", None),
        P(None, "fsdp"),
    )
    out_specs = (
        P(("rep", "fsdp"), None),
        P(("rep", "fsdp"), None),
        P(None, "fsdp"),
        P(None, "fsdp"),
        P(None, "fsdp", None),
        P(None, "fsdp"),
        P(None, "fsdp"),
        P(None, "fsdp", None),
        P(None, "fsdp"),
        P(None, "fsdp"),
        P(None, "fsdp"),
        P(None, "fsdp", None),
        P(None, "fsdp"),
        P(None, "fsdp", None),
        P(None, "fsdp"),
    )
    return jax.shard_map(local, mesh=mesh, in_specs=in_specs, out_specs=out_specs, check_vma=False)
```

profile of v0, /device:TPU:0, one launch (start us, length us, event | category | flops | bytes accessed | tf_op | source)
XLA Modules:
  0.0 1005.3 jit_solution(12111125069816792408)
XLA Ops:
  28.2 26.4 %all-reduce.20 = (bf16[384]{0:T(512)(128)(2,1)}, bf16[384]{0:T(512)(128)(2,1)S(1)}, bf16[384]{0:T(512)(128)(2,1)S(1)}, bf16[384]{0:T(512)(128)(2,1)S(1)}, bf16[3...) all-reduce(bf16[384]{0:T(512)(128)(2,1)S(1)} %dynamic-update-slice., ...), channel_id=8, replica_groups=mesh['rep'=4,'fsdp'=8] {'fsdp'}, use_global_device_ids=true, to_apply=%add.4 | all-reduce | flops 9216 | bytes 36864
  55.3 11.4 %all-gather.2 = bf16[1,384,1152]{2,1,0:T(8,128)(2,1)S(1)} all-gather(bf16[1,48,1152]{2,1,0:T(8,128)(2,1)S(1)} %get-tuple-element.133), channel_id=4, replica_groups=mesh['rep'=4,'fsdp'=8] {'fsdp'}, dimensions={1}, use_global_device_ids=true | all-gather | bytes 995328 | tf_op jit(solution)/shard_map/all_gather | solution.py:252
  108.4 10.5 %all-gather.18 = bf16[1,384,384]{2,1,0:T(8,128)(2,1)} all-gather(bf16[1,48,384]{2,1,0:T(8,128)(2,1)S(1)} %get-tuple-element.134), channel_id=20, replica_groups=mesh['rep'=4,'fsdp'=8] {'fsdp'}, dimensions={1}, use_global_device_ids=true | all-gather | bytes 331776 | tf_op jit(solution)/shard_map/all_gather | solution.py:255
  118.9 9.8 all-gather.5
  128.7 10.3 %all-gather.15 = bf16[1,384,1152]{2,1,0:T(8,128)(2,1)S(1)} all-gather(bf16[1,48,1152]{2,1,0:T(8,128)(2,1)S(1)} %copy-done.76), channel_id=17, replica_groups=mesh['rep'=4,'fsdp'=8] {'fsdp'}, dimensions={1}, use_global_device_ids=true | all-gather | bytes 995328 | tf_op jit(solution)/shard_map/all_gather | solution.py:252
  145.6 7.1 multiply_convert_fusion.5
  196.3 6.6 multiply_convert_fusion.4
  203.0 7.0 fusion.131
  223.8 11.2 %multiply_reduce_fusion.3 = (f32[6,512]{1,0:T(8,128)S(1)}, f32[6,512,1024]{2,1,0:T(8,128)}) fusion(f32[6,512,1024]{2,1,0:T(8,128)} %copy-done, f32[6,512]{1,0:T(8,128)S(1)} %log_add_fusion.3, pred[512,1024]{1,0:T(8,128)(4,1)S(1)} %get-tuple-element.136, bf16[512,6,64]{0,2,1:T(8,128)(2,1)S(1)} %bitcast.262, bf16[1024,6,64]{0,2,1:T(8,128)(2,1)S(1)} %bitcast.249), kind=kOutput, calls=%fused_computation.10 | convolution fusion | flops 415233024 | bytes 26894336 | tf_op jit(solution)/shard_map/qhd,khd->hqk/dot_general | solution.py:97
  236.6 10.6 %multiply_convert_fusion.3 = bf16[6,512,1024]{2,1,0:T(8,128)(2,1)} fusion(f32[6,512,1024]{2,1,0:T(8,128)} %get-tuple-element.177, f32[6,512,1024]{2,1,0:T(8,128)S(1)} %bitcast.229, f32[6,512]{1,0:T(8,128)S(1)} %get-tuple-element.176, f32[6,512]{1,0:T(8,128)S(1)} %log_add_fusion.3, pred[512,1024]{1,0:T(8,128)(4,1)S(1)} %get-tuple-element.136), kind=kLoop, calls=%fused_computation.9 | loop fusion | flops 15728640 | bytes 32006144 | tf_op jit(solution)/shard_map/convert_element_type | solution.py:101
  262.4 8.0 multiply_reduce_fusion.2
  278.4 10.0 multiply_convert_fusion.2
  308.3 7.2 fusion.132
  328.5 7.5 fusion.8
  336.0 10.4 %multiply_reduce_fusion = (f32[6,512]{1,0:T(8,128)}, f32[6,512,1024]{2,1,0:T(8,128)}) fusion(f32[6,512,1024]{2,1,0:T(8,128)} %copy-done.3, f32[6,512]{1,0:T(8,128)S(1)} %copy-done.80, pred[512,1024]{1,0:T(8,128)(4,1)S(1)} %get-tuple-element.137, bf16[512,6,64]{0,2,1:T(8,128)(2,1)S(1)} %bitcast.267, bf16[1024,6,64]{0,2,1:T(8,128)(2,1)S(1)} %bitcast.244), kind=kOutput, calls=%fused_computation.1 | convolution fusion | flops 415233024 | bytes 26894336 | tf_op jit(solution)/shard_map/qhd,khd->hqk/dot_general | solution.py:97
  346.4 7.8 multiply_reduce_fusion.1
  354.2 16.2 %multiply_convert_fusion = (bf16[6,512,1024]{2,1,0:T(8,128)(2,1)}, bf16[6,512,1024]{2,1,0:T(8,128)(2,1)S(1)}) fusion(f32[6,512,1024]{2,1,0:T(8,128)} %get-tuple-element.185, f32[6,512,1024]{2,1,0:T(8,128)} %copy-done.3, f32[6,512]{1,0:T(8,128)} %get-tuple-element.184, f32[6,512]{1,0:T(8,128)} %log_add_fusion, pred[512,1024]{1,0:T(8,128)(4,1)} %copy-done.6, ...), kind=kLoop, calls=%fused_computation | loop fusion | flops 31457280 | bytes 64012288 | tf_op jit(solution)/shard_map/convert_element_type | solution.py:101
  378.9 8.0 bitcast_convert_fusion
  449.1 17.4 %reduce-scatter.32.cloned.1.call-done = f32[2,48,1152]{2,1,0:T(8,128)} async-done(((f32[2,384,1152]{2,1,0:T(8,128)}), f32[2,48,1152]{2,1,0:T(8,128)}) %reduce-scatter.32.cloned.1.call-update) | async-done | bytes 442384 | tf_op jit(solution)/shard_map/reduce_scatter | solution.py:339
  466.5 57.2 %reduce-scatter.38.cloned.1.call-done = f32[2,192,384]{2,1,0:T(8,128)} async-done(((f32[2,1536,384]{2,1,0:T(8,128)}), f32[2,192,384]{2,1,0:T(8,128)}) %reduce-scatter.38.cloned.1.call-update) | async-done | bytes 589840 | tf_op jit(solution)/shard_map/reduce_scatter | solution.py:348
  523.7 57.2 %reduce-scatter.36.cloned.1.call-done = f32[2,48,1536]{2,1,0:T(8,128)} async-done(((f32[2,384,1536]{2,1,0:T(8,128)}), f32[2,48,1536]{2,1,0:T(8,128)}) %reduce-scatter.36.cloned.1.call-update) | async-done | bytes 589840 | tf_op jit(solution)/shard_map/reduce_scatter | solution.py:346
  595.0 22.6 %reduce-scatter.56.cloned.1.call-done = f32[48,2]{1,0:T(8,128)} async-done(((f32[384,2]{1,0:T(8,128)}), f32[48,2]{1,0:T(8,128)}) %reduce-scatter.56.cloned.1.call-update) | async-done | bytes 400
  618.4 35.7 %reduce-scatter.52.cloned.1.call-done = f32[48,2]{1,0:T(8,128)} async-done(((f32[384,2]{1,0:T(8,128)}), f32[48,2]{1,0:T(8,128)}) %reduce-scatter.52.cloned.1.call-update) | async-done | bytes 400
  655.0 35.9 %reduce-scatter.48.cloned.1.call-done = f32[48,2]{1,0:T(8,128)} async-done(((f32[384,2]{1,0:T(8,128)}), f32[48,2]{1,0:T(8,128)}) %reduce-scatter.48.cloned.1.call-update) | async-done | bytes 400
  691.7 35.7 %reduce-scatter.50.cloned.1.call-done = f32[48,2]{1,0:T(8,128)} async-done(((f32[384,2]{1,0:T(8,128)}), f32[48,2]{1,0:T(8,128)}) %reduce-scatter.50.cloned.1.call-update) | async-done | bytes 400
  728.2 35.9 %reduce-scatter.46.cloned.1.call-done = f32[48,2]{1,0:T(8,128)} async-done(((f32[384,2]{1,0:T(8,128)}), f32[48,2]{1,0:T(8,128)}) %reduce-scatter.46.cloned.1.call-update) | async-done | bytes 400
  764.9 36.3 %reduce-scatter.44.cloned.1.call-done = f32[48,2]{1,0:T(8,128)} async-done(((f32[384,2]{1,0:T(8,128)}), f32[48,2]{1,0:T(8,128)}) %reduce-scatter.44.cloned.1.call-update) | async-done | bytes 400
  802.1 36.3 %reduce-scatter.42.cloned.1.call-done = f32[48,2]{1,0:T(8,128)} async-done(((f32[384,2]{1,0:T(8,128)}), f32[48,2]{1,0:T(8,128)}) %reduce-scatter.42.cloned.1.call-update) | async-done | bytes 400
  839.2 36.3 %reduce-scatter.40.cloned.1.call-done = f32[48,2]{1,0:T(8,128)} async-done(((f32[384,2]{1,0:T(8,128)}), f32[48,2]{1,0:T(8,128)}) %reduce-scatter.40.cloned.1.call-update) | async-done | bytes 400
  876.3 37.1 %reduce-scatter.54.cloned.1.call-done = f32[192,2]{1,0:T(8,128)} async-done(((f32[1536,2]{1,0:T(8,128)}), f32[192,2]{1,0:T(8,128)}) %reduce-scatter.54.cloned.1.call-update) | async-done | bytes 1552
  914.5 20.2 %all-reduce.18 = (f32[2,48]{1,0:T(2,128)}, f32[2,48]{1,0:T(2,128)}, f32[2,48]{1,0:T(2,128)}, f32[2,48]{1,0:T(2,128)}, f32[2,48]{1,0:T(2,128)}, /*index=5*/f32[2,...) all-reduce(f32[2,48]{1,0:T(2,128)S(1)} %copy.143, ...), channel_id=1, replica_groups=mesh['rep'=4,'fsdp'=8] {'rep'}, use_global_device_ids=true, to_apply=%region_31.32 | all-reduce | flops 1152 | bytes 9216 | tf_op jit(solution)/shard_map/psum | solution.py:351
  934.7 57.1 %all-reduce.23.cloned.1.call-done = (f32[2,48,1152]{2,1,0:T(8,128)}, f32[2,48,384]{2,1,0:T(8,128)}, f32[2,48,1536]{2,1,0:T(8,128)}, f32[2,192,384]{2,1,0:T(8,128)}) async-done(((f32[2,48,1152]{2,1,0:T(8,128)}, f32[2,48,384]{2,1,0:T(8,128)}, f32[2,48,1536]{2,1,0:T(8,128)}, f32[2,192,384]{2,1,0:T(8,128)}), (f32[2,48,1152]{2,1,0:T(8,128)}, f32[2,48,384]{2,1,0:T(8,128)}, f32[2,48,1536]{2,1,0:T(8,128)}, ...) | async-done | bytes 1769488 | tf_op jit(solution)/shard_map/psum | solution.py:351
  (595 shorter events, 280.1 us)
Async XLA Ops:
  7.2 138.4 %all-gather.31.cloned.1.call-start = ((), (), s32[]{:S(2)}) async-start(), calls=%async_computation.17 | async-start | bytes 1327104 | tf_op jit(solution)/shard_map/all_gather | solution.py:259
  9.1 143.7 %all-gather.33.cloned.1.call-start = ((), (), s32[]{:S(2)}) async-start(), calls=%async_computation.18 | async-start | bytes 1327104 | tf_op jit(solution)/shard_map/all_gather | solution.py:261
  10.9 185.4 %all-gather.35.cloned.1.call-start = ((), (), s32[]{:S(2)}) async-start(), calls=%async_computation.19 | async-start | bytes 1327104 | tf_op jit(solution)/shard_map/all_gather | solution.py:259
  11.6 191.3 %all-gather.37.cloned.1.call-start = ((), (), s32[]{:S(2)}) async-start(), calls=%async_computation.20 | async-start | bytes 1327104 | tf_op jit(solution)/shard_map/all_gather | solution.py:261
  12.2 436.9 %reduce-scatter.34.cloned.1.call-start = ((), (), s32[]{:S(2)}) async-start(), calls=%async_computation.14 | async-start | bytes 1327104 | tf_op jit(solution)/shard_map/reduce_scatter | solution.py:342
  23.5 31.2 %copy-start.81 = (bf16[2,48,1152]{2,1,0:T(8,128)(2,1)S(1)}, bf16[2,48,1152]{2,1,0:T(8,128)(2,1)}, u32[]{:S(2)}) copy-start(bf16[2,48,1152]{2,1,0:T(8,128)(2,1)} %param.21) | copy-start | bytes 663556
  24.0 118.4 %copy-start.4 = (f32[1024,384]{0,1:T(8,128)}, f32[1024,384]{0,1:T(8,128)S(1)}, u32[]{:S(2)}) copy-start(f32[1024,384]{0,1:T(8,128)S(1)} %copy.114) | copy-start | bytes 4718596
  24.2 44.4 %copy-start.78 = (f32[1024]{0:T(1024)}, f32[1024]{0:T(1024)S(1)}, u32[]{:S(2)}) copy-start(f32[1024]{0:T(1024)S(1)} %broadcast_multiply_fusion.11) | copy-start | bytes 12292
  81.6 254.4 %copy-start.6 = (pred[512,1024]{1,0:T(8,128)(4,1)}, pred[512,1024]{1,0:T(8,128)(4,1)S(1)}, u32[]{:S(2)}) copy-start(pred[512,1024]{1,0:T(8,128)(4,1)S(1)} %get-tuple-element.137) | copy-start | bytes 1572868
  101.2 27.5 %copy-start.76 = (bf16[1,48,1152]{2,1,0:T(8,128)(2,1)S(1)}, bf16[1,48,1152]{2,1,0:T(8,128)(2,1)}, u32[]{:S(2)}) copy-start(bf16[1,48,1152]{2,1,0:T(8,128)(2,1)} %get-tuple-element.132) | copy-start | bytes 331780
  106.0 39.6 %copy-start.102 = (f32[384]{0:T(512)}, f32[384]{0:T(512)S(1)}, u32[]{:S(2)}) copy-start(f32[384]{0:T(512)S(1)} %convert_element_type.275) | copy-start | bytes 4612
  106.0 200.9 %copy-start.92 = (f32[384]{0:T(512)}, f32[384]{0:T(512)S(1)}, u32[]{:S(2)}) copy-start(f32[384]{0:T(512)S(1)} %convert_element_type.279) | copy-start | bytes 4612
  106.0 113.4 %copy-start.105 = (f32[384]{0:T(512)}, f32[384]{0:T(512)S(1)}, u32[]{:S(2)}) copy-start(f32[384]{0:T(512)S(1)} %convert_element_type.284) | copy-start | bytes 4612
  106.6 50.6 %copy-start.107 = (f32[384]{0:T(512)}, f32[384]{0:T(512)S(1)}, u32[]{:S(2)}) copy-start(f32[384]{0:T(512)S(1)} %convert_element_type.280) | copy-start | bytes 4612
  107.8 37.8 %copy-start.120 = (f32[1536]{0:T(1024)}, f32[1536]{0:T(1024)S(1)}, u32[]{:S(2)}) copy-start(f32[1536]{0:T(1024)S(1)} %convert_element_type.277) | copy-start | bytes 18436
  156.9 37.2 %copy-start.7 = (f32[1024,384]{0,1:T(8,128)}, f32[1024,384]{0,1:T(8,128)S(1)}, u32[]{:S(2)}) copy-start(f32[1024,384]{0,1:T(8,128)S(1)} %get-tuple-element.165) | copy-start | bytes 4718596
  194.8 24.6 %copy-start.88 = (f32[1024]{0:T(1024)}, f32[1024]{0:T(1024)S(1)}, u32[]{:S(2)}) copy-start(f32[1024]{0:T(1024)S(1)} %broadcast_multiply_fusion.8) | copy-start | bytes 12292
  196.2 23.2 %copy-start.98 = (f32[1024]{0:T(1024)}, f32[1024]{0:T(1024)S(1)}, u32[]{:S(2)}) copy-start(f32[1024]{0:T(1024)S(1)} %add_rsqrt_fusion) | copy-start | bytes 12292
  378.2 88.4 %reduce-scatter.32.cloned.1.call-start = ((), (), s32[]{:S(2)}) async-start(), calls=%async_computation.13 | async-start | bytes 3981312 | tf_op jit(solution)/shard_map/reduce_scatter | solution.py:339
  409.5 114.2 %reduce-scatter.38.cloned.1.call-start = ((), (), s32[]{:S(2)}) async-start(), calls=%async_computation.16 | async-start | bytes 5308416 | tf_op jit(solution)/shard_map/reduce_scatter | solution.py:348
  418.5 162.4 %reduce-scatter.36.cloned.1.call-start = ((), (), s32[]{:S(2)}) async-start(), calls=%async_computation.15 | async-start | bytes 5308416 | tf_op jit(solution)/shard_map/reduce_scatter | solution.py:346
  427.6 190.0 %reduce-scatter.56.cloned.1.call-start = ((), (), s32[]{:S(2)}) async-start(), calls=%async_computation.29 | async-start | bytes 221184
  440.9 213.2 %reduce-scatter.52.cloned.1.call-start = ((), (), s32[]{:S(2)}) async-start(), calls=%async_computation.27 | async-start | bytes 221184
  441.9 249.0 %reduce-scatter.48.cloned.1.call-start = ((), (), s32[]{:S(2)}) async-start(), calls=%async_computation.25 | async-start | bytes 221184
  442.9 284.6 %reduce-scatter.50.cloned.1.call-start = ((), (), s32[]{:S(2)}) async-start(), calls=%async_computation.26 | async-start | bytes 221184
  443.9 320.2 %reduce-scatter.46.cloned.1.call-start = ((), (), s32[]{:S(2)}) async-start(), calls=%async_computation.24 | async-start | bytes 221184
  444.9 136.1 %copy-start.132 = (bf16[384]{0:T(512)(128)(2,1)S(1)}, bf16[384]{0:T(512)(128)(2,1)}, u32[]{:S(2)}) copy-start(bf16[384]{0:T(512)(128)(2,1)} %get-tuple-element.104) | copy-start | bytes 2308
  444.9 356.4 %reduce-scatter.44.cloned.1.call-start = ((), (), s32[]{:S(2)}) async-start(), calls=%async_computation.23 | async-start | bytes 221184
  445.8 392.6 %reduce-scatter.42.cloned.1.call-start = ((), (), s32[]{:S(2)}) async-start(), calls=%async_computation.22 | async-start | bytes 221184
  446.8 428.8 %reduce-scatter.40.cloned.1.call-start = ((), (), s32[]{:S(2)}) async-start(), calls=%async_computation.21 | async-start | bytes 221184
  447.7 465.8 %reduce-scatter.54.cloned.1.call-start = ((), (), s32[]{:S(2)}) async-start(), calls=%async_computation.28 | async-start | bytes 884736
  449.0 542.8 %all-reduce.23.cloned.1.call-start = ((), (), s32[]{:S(2)}) async-start(), calls=%async_computation.30 | async-start | bytes 3538944 | tf_op jit(solution)/shard_map/psum | solution.py:351
  (144 other events, 716.7 us)
Sparse Core Ops, SparseCore 0:
  10.5 26.6 all-gather.30
  39.6 25.0 all-gather.32
  67.2 23.9 all-gather.34
  92.9 24.3 all-gather.36
  378.3 36.9 reduce-scatter.33
  418.6 47.8 reduce-scatter.31
  470.0 53.7 reduce-scatter.37
  527.2 53.7 reduce-scatter.35
  584.0 33.6 reduce-scatter.55
  620.5 33.6 reduce-scatter.51
  657.2 33.6 reduce-scatter.47
  693.8 33.6 reduce-scatter.49
  730.4 33.6 reduce-scatter.45
  767.6 33.6 reduce-scatter.43
  804.7 33.6 reduce-scatter.41
  841.9 33.6 reduce-scatter.39
  878.5 34.9 reduce-scatter.53
  916.0 75.7 all-reduce.22
where the time goes:
time: 1010 us
  waiting for transfers between devices  502 us (50%)
  matrix products  199 us (20%)
  local copies, waits for them, and re-layouts  101 us (10%)
  other arithmetic  94.8 us (9%)
  blocking collectives  88.6 us (9%)
  between operations  18 us (2%)
    unnamed x27, waiting for transfers between devices  313 us
    dot_general x24, matrix products, matmul(): return jnp.dot(left, right, preferred_element_type=jnp.float32)  77.2 us
    reduce_scatter x1, waiting for transfers between devices, local(): lax.psum_scatter(stacked[9], 'fsdp', scatter_dimension=1, tiled=True)  57.2 us
    reduce_scatter x1, waiting for transfers between devices, local(): lax.psum_scatter(stacked[11], 'fsdp', scatter_dimension=1, tiled=True)  57.2 us
    psum x1, waiting for transfers between devices, local(): lax.psum((shard_sums[0], shard_sums[1], shard_sums[2], shard_sums[3], sha...  57.1 us
    unnamed x387, local copies, waits for them, and re-layouts  55.7 us
    dot_general x4, matrix products, attend_backward(): jnp.einsum('qhd,khd->hqk', grad_blk, value3, preferred_element_type=jnp.f...  37.5 us
    convert_element_type x3, other arithmetic, attend_backward(): grad_scores = (probs * (grad_probs - delta)).astype(jnp.bfloat16)  36.8 us
  transfers between devices with their start and end apart: 18, of which 13 were waited for; matrix products, arithmetic and copies ran while one was open for 20% of the time, Pallas kernels for 0%

commit v1 on v0

v1 whole, which is shorter than its diff:
```python
import functools
from types import SimpleNamespace as NS
import jax
import jax.numpy as jnp
from jax import lax
from jax.experimental import pallas as pl
from jax.experimental.pallas import tpu as pltpu

HEADS = 6
HEAD_DIM = 64
IMG = 197
STEP = 192
QWIN = 224
KWIN = 256
TILE = 256
norm_eps = 1e-06
neg_fill = -1e30
root_half = 0.7071067811865476
inv_root_tau = 0.3989422804014327
F32, BF16 = jnp.float32, jnp.bfloat16


def nn(a, b):
    return lax.dot_general(a, b, (((1,), (0,)), ((), ())), preferred_element_type=F32)


def nt(a, b):
    return lax.dot_general(a, b, (((1,), (1,)), ((), ())), preferred_element_type=F32)


def tn(a, b):
    return lax.dot_general(a, b, (((0,), (0,)), ((), ())), preferred_element_type=F32)


def fold8(x):
    return jnp.sum(x.reshape(x.shape[0] // 8, 8, x.shape[1]), axis=0)


def norm(x):
    c = x - jnp.mean(x, -1, keepdims=True)
    r = lax.rsqrt(jnp.mean(c * c, -1, keepdims=True) + norm_eps)
    return c * r, r


def norm_back(grad, n, r, gain):
    e = grad * gain
    return r * (e - jnp.mean(e, -1, keepdims=True) - n * jnp.mean(e * n, -1, keepdims=True))


def gelu_both(pre):
    cdf = 0.5 * (1.0 + lax.erf(pre * root_half))
    return pre * cdf, cdf + pre * jnp.exp(-0.5 * pre * pre) * inv_root_tau


def vrow(R, l, k):
    return R.vec[12 * l + k : 12 * l + k + 1, :]


def add_sum(R, l, k, x):
    R.vacc[12 * l + k] += fold8(x)


def stage_qkv(R, l, src):
    gain, bias, qb, vb = (vrow(R, l, k) for k in range(4))

    def tile(i, c):
        rows = pl.ds(pl.multiple_of(i * TILE, TILE), TILE)
        n, r = norm(src[rows, :])
        R.n1[l, rows, :] = n
        R.stats[l, rows, 0:1] = r
        a = (n * gain + bias).astype(BF16)
        R.aT[l, :, rows] = a.T
        proj = nn(a, R.wqkv[l])
        R.q[l, rows, :] = ((proj[:, :384] + qb) * (HEAD_DIM**-0.5)).astype(BF16)
        R.k[l, rows, :] = proj[:, 384:768].astype(BF16)
        R.v[l, rows, :] = (proj[:, 768:] + vb).astype(BF16)
        return c

    lax.fori_loop(0, R.rows // TILE, tile, 0)


def stack_heads(x, low):
    zero = jnp.zeros_like(x)
    return jnp.concatenate([jnp.where(low, x, zero), jnp.where(low, zero, x)], 0)


def attend(q, k, v, bias):
    n = q.shape[0]
    low = lax.broadcasted_iota(jnp.int32, (1, 128), 1) < HEAD_DIM
    s = nt(stack_heads(q, low), k)
    if bias.shape[0] == n:
        bias = jnp.concatenate([bias, bias], 0)
    s = s + bias
    top = jnp.max(s, -1, keepdims=True)
    p = jnp.exp(s - top)
    den = jnp.sum(p, -1, keepdims=True)
    o = nn((p * (1.0 / den)).astype(BF16), v)
    return jnp.where(low, o[:n], o[n:]).astype(BF16), top + jnp.log(den)


def stage_attend(R, l):
    def put(pr, start, first, o, lse):
        n = o.shape[0]
        lanes = slice(128 * pr, 128 * pr + 128)
        head = pl.ds(start, 32)
        rest = pl.ds(start + 32, n - 32)
        old = start + lax.broadcasted_iota(jnp.int32, (32, 1), 0) < first
        R.att[head, lanes] = jnp.where(old, R.att[head, lanes].astype(F32), o[:32].astype(F32)).astype(BF16)
        R.att[rest, lanes] = o[32:]
        for h in range(2):
            col = slice(2 + 2 * pr + h, 3 + 2 * pr + h)
            R.stats[l, head, col] = jnp.where(old, R.stats[l, head, col], lse[n * h : n * h + 32])
            R.stats[l, rest, col] = lse[n * h + 32 : n * h + n]

    def window(j, c):
        start = pl.multiple_of(j * STEP, STEP)
        col = lax.broadcasted_iota(jnp.int32, (1, KWIN), 1)
        bias = jnp.where((col >= 5 * j) & (col < 5 * j + IMG), 0.0, neg_fill)
        for pr in range(3):
            lanes = slice(128 * pr, 128 * pr + 128)
            o, lse = attend(
                R.q[l, pl.ds(start, QWIN), lanes], R.k[l, pl.ds(start, KWIN), lanes],
                R.v[l, pl.ds(start, KWIN), lanes], bias)
            put(pr, start, IMG * j, o, lse)
        return c

    lax.fori_loop(0, 2, window, 0)

    def rest(t, c):
        start = pl.multiple_of(2 * STEP + t * 128, 128)
        bias = R.segbias[pl.ds(pl.multiple_of(t * 128, 128), 128), :]
        for pr in range(3):
            lanes = slice(128 * pr, 128 * pr + 128)
            o, lse = attend(
                R.q[l, pl.ds(start, 128), lanes], R.k[l, 2 * STEP :, lanes],
                R.v[l, 2 * STEP :, lanes], bias)
            put(pr, start, 2 * IMG, o, lse)
        return c

    lax.fori_loop(0, (R.rows - 2 * STEP) // 128, rest, 0)


def stage_mlp(R, l, src, dst):
    ob, gain, bias, db = (vrow(R, l, k) for k in (4, 5, 6, 7))

    def tile(i, c):
        rows = pl.ds(pl.multiple_of(i * TILE, TILE), TILE)
        att = R.att[rows, :]
        R.attT[l, :, rows] = att.T
        mid = src[rows, :] + nn(att, R.wo[l]) + ob
        n, r = norm(mid)
        R.n2[l, rows, :] = n
        R.stats[l, rows, 1:2] = r
        m = (n * gain + bias).astype(BF16)
        R.mT[l, :, rows] = m.T
        acc = mid + db
        for ch in range(4):
            cols = slice(384 * ch, 384 * ch + 384)
            pre = nn(m, R.wup[l, :, cols]) + vrow(R, l, 8 + ch)
            hid, slope = gelu_both(pre)
            hid = hid.astype(BF16)
            R.hidT[l, cols, rows] = hid.T
            R.slope[l, rows, cols] = slope.astype(BF16)
            acc = acc + nn(hid, R.wd[l, cols, :])
        dst[rows, :] = acc
        return c

    lax.fori_loop(0, R.rows // TILE, tile, 0)


def stage_mlp_back(R, l):
    gain = vrow(R, l, 5)

    def tile(i, c):
        rows = pl.ds(pl.multiple_of(i * TILE, TILE), TILE)
        g = R.g[rows, :]
        gl = g.astype(BF16)
        R.gl[rows, :] = gl
        add_sum(R, l, 7, g)
        dm = jnp.zeros_like(g)
        for ch in range(4):
            cols = slice(384 * ch, 384 * ch + 384)
            dpre = nt(gl, R.wd[l, cols, :]) * R.slope[l, rows, cols].astype(F32)
            add_sum(R, l, 8 + ch, dpre)
            dpre = dpre.astype(BF16)
            R.slope[l, rows, cols] = dpre
            dm = dm + nt(dpre, R.wup[l, :, cols])
        n = R.n2[l, rows, :]
        add_sum(R, l, 5, dm * n)
        add_sum(R, l, 6, dm)
        gm = g + norm_back(dm, n, R.stats[l, rows, 1:2], gain)
        add_sum(R, l, 4, gm)
        R.g[rows, :] = gm
        gml = gm.astype(BF16)
        R.gml[rows, :] = gml
        R.datt[rows, :] = nt(gml, R.wo[l]).astype(BF16)
        return c

    lax.fori_loop(0, R.rows // TILE, tile, 0)


def stage_weight_down(R, l):
    def block(b, c):
        rows = pl.ds(pl.multiple_of(b * n, n), n)
        R.grad(0, l)[lax.rem(b, 2), b // 2] = nn(R.hidT[l, rows, :], R.gl[...]).astype(BF16)
        return c

    n = R.hidT.shape[1] // 8
    lax.fori_loop(0, 8, block, 0)


def put_rows(ref, cols, x):
    n = x.shape[0] // 8
    for b in range(8):
        ref[b % 2, b // 2, :, cols] = x[n * b : n * b + n].astype(BF16)


def stage_weight_up(R, l):
    def block(b, c):
        cols = pl.ds(pl.multiple_of(b * 256, 256), 256)
        put_rows(R.grad(1, l), cols, nn(R.mT[l], R.slope[l, :, cols]))
        return c

    lax.fori_loop(0, 6, block, 0)


def stage_weight_out(R, l):
    put_rows(R.grad(2, l), slice(1152, 1536), nn(R.attT[l], R.gml[...]))


def stage_weight_qkv(R, l):
    def block(b, c):
        cols = pl.ds(pl.multiple_of(b * 384, 128), 384)
        put_rows(R.grad(2, l), cols, nn(R.aT[l], R.dproj[:, cols]))
        return c

    lax.fori_loop(0, 3, block, 0)


def stage_attend_back(R, l):
    R.dproj[...] = jnp.zeros(R.dproj.shape, BF16)
    low = lax.broadcasted_iota(jnp.int32, (1, 128), 1) < HEAD_DIM

    def put(start, col, x):
        n = x.shape[0]
        head = pl.ds(start, 32)
        lanes = slice(col, col + 128)
        R.dproj[head, lanes] = (R.dproj[head, lanes].astype(F32) + x[:32]).astype(BF16)
        R.dproj[pl.ds(start + 32, n - 32), lanes] = x[32:].astype(BF16)

    def window(j, c):
        start = pl.multiple_of(j * STEP, STEP)
        qrows, krows = pl.ds(start, QWIN), pl.ds(start, KWIN)
        col = lax.broadcasted_iota(jnp.int32, (1, KWIN), 1)
        colbias = jnp.where((col >= 5 * j) & (col < 5 * j + IMG), 0.0, neg_fill)
        row = lax.broadcasted_iota(jnp.int32, (QWIN, 1), 0)
        rowin = (row >= 5 * j) & (row < 5 * j + IMG)
        for pr in range(3):
            lanes = slice(128 * pr, 128 * pr + 128)
            q01 = stack_heads(R.q[l, qrows, lanes], low)
            do01 = stack_heads(R.datt[qrows, lanes], low)
            k, v = R.k[l, krows, lanes], R.v[l, krows, lanes]
            lse01 = jnp.concatenate(
                [jnp.where(rowin, R.stats[l, qrows, c : c + 1], -neg_fill) for c in (2 + 2 * pr, 3 + 2 * pr)], 0)
            p = jnp.exp((nt(q01, k) - lse01) + colbias)
            pdp = nt(do01, v)
            delta = jnp.sum(p * pdp, -1, keepdims=True)
            ds = (p * (pdp - delta)).astype(BF16)
            dq01 = nn(ds, k)
            dq = jnp.where(low, dq01[:QWIN], dq01[QWIN:]) * (HEAD_DIM**-0.5)
            dk = tn(ds, q01)[:QWIN]
            dv = tn(p.astype(BF16), do01)[:QWIN]
            put(start, 128 * pr, dq)
            put(start, 384 + 128 * pr, dk)
            put(start, 768 + 128 * pr, dv)
            R.vacc[12 * l + 2, :, lanes] += fold8(dq)
            R.vacc[12 * l + 3, :, lanes] += fold8(dv)
        return c

    lax.fori_loop(0, 5, window, 0)


def stage_qkv_back(R, l):
    gain = vrow(R, l, 0)

    def tile(i, c):
        rows = pl.ds(pl.multiple_of(i * TILE, TILE), TILE)
        da = nt(R.dproj[rows, :], R.wqkv[l])
        n = R.n1[l, rows, :]
        add_sum(R, l, 0, da * n)
        add_sum(R, l, 1, da)
        R.g[rows, :] = R.g[rows, :] + norm_back(da, n, R.stats[l, rows, 0:1], gain)
        return c

    lax.fori_loop(0, R.rows // TILE, tile, 0)


def stage_segments(R):
    seg = R.seg[...].astype(F32)
    cols = jnp.broadcast_to(seg, (128, R.rows)).T
    R.segcol[...] = cols
    keys = seg[:, 2 * STEP :]

    def tile(t, c):
        rows = pl.ds(pl.multiple_of(t * 128, 128), 128)
        mine = R.segcol[pl.ds(pl.multiple_of(2 * STEP + t * 128, 128), 128), :1]
        R.segbias[rows, :] = jnp.where(mine == keys, 0.0, neg_fill)
        return c

    lax.fori_loop(0, (R.rows - 2 * STEP) // 128, tile, 0)


def stage_cotangent(R):
    def tile(i, c):
        rows = pl.ds(pl.multiple_of(i * TILE, TILE), TILE)
        R.g[rows, :] = jnp.where(R.segcol[rows, :1] >= 0.0, R.cot[rows, :], 0.0)
        return c

    lax.fori_loop(0, R.rows // TILE, tile, 0)


def compute(R, streams, hook):
    R.vacc[...] = jnp.zeros(R.vacc.shape, F32)
    stage_segments(R)
    for l in range(2):
        hook("qkv", l)
        stage_qkv(R, l, streams[l])
        hook("att", l)
        stage_attend(R, l)
        hook("mlp", l)
        stage_mlp(R, l, streams[l], streams[l + 1])
    hook("fwd", 0)
    stage_cotangent(R)
    for l in (1, 0):
        stage_mlp_back(R, l)
        hook("b0", l)
        stage_weight_down(R, l)
        hook("dD", l)
        stage_weight_up(R, l)
        hook("dU", l)
        stage_weight_out(R, l)
        hook("dO", l)
        stage_attend_back(R, l)
        hook("batt", l)
        stage_weight_qkv(R, l)
        hook("dA", l)
        stage_qkv_back(R, l)
        hook("b1", l)


MESH = pl.DeviceIdType.MESH
VECTORS = 8


def scratch_single(rows, d, f):
    v = pltpu.VMEM
    return dict(
        mid=v((rows, d), F32), n1=v((2, rows, d), F32), n2=v((2, rows, d), F32),
        stats=v((2, rows, 128), F32), aT=v((2, d, rows), BF16),
        q=v((2, rows, d), BF16), k=v((2, rows, d), BF16), v=v((2, rows, d), BF16),
        att=v((rows, d), BF16), attT=v((2, d, rows), BF16), mT=v((2, d, rows), BF16),
        hidT=v((2, f, rows), BF16), slope=v((2, rows, f), BF16),
        segcol=v((rows, 128), F32), segbias=v((rows - 2 * STEP, rows - 2 * STEP), F32),
        gl=v((rows, d), BF16), gml=v((rows, d), BF16),
        dproj=v((rows, 3 * d), BF16), vacc=v((24, 8, d), F32),
    )


def scratch_comm(d, f):
    v, dma = pltpu.VMEM, pltpu.SemaphoreType.DMA
    s, t = d // 8, f // 8
    return dict(
        wqkv=v((2, d, 3 * d), BF16), wo=v((2, d, d), BF16), wup=v((2, d, f), BF16), wd=v((2, f, d), BF16),
        pk=v((24, 128), F32), mine=v((24, d), F32), gat=v((8, 24, d), F32), vec=v((24, d), F32),
        dD=v((2, 4, t, d), BF16), dU=v((2, 4, s, f), BF16), dA=v((2, 4, s, f), BF16),
        pD=v((2, 4, t, d), BF16), pU=v((2, 4, s, f), BF16), pA=v((2, 4, s, f), BF16),
        xD=v((2, 3, t, d), BF16), xU=v((2, 3, s, f), BF16), xA=v((2, 3, s, f), BF16),
        zb=v((6, 4, s, d), BF16), zr=v((6, 4, s, d), BF16),
        v0=v((2, 12, d), F32), v1=v((2, 12, d), F32), v2=v((2, 12, d), F32), v3=v((2, 3, 12, d), F32), v4=v((2, 4, 12, d), F32),
        loc=dma((9,)), ags=dma((9, 7)), agr=dma((9, 7)), s1s=dma((8,)), s1r=dma((8,)), s2s=dma((8, 3)), s2r=dma((8, 3)),
        s3s=dma((8, 3)), s3r=dma((8, 3)), s4s=dma((6, 3)), s4r=dma((6, 3)),
    )


class Comm:
    def __init__(self, R):
        self.R = R
        self.f = lax.axis_index("fsdp")
        self.z = lax.axis_index("rep")
        f = self.f
        self.c = lax.rem(f, 2)
        self.p = f // 2
        dx = 1 - 2 * lax.rem(self.p, 2)
        dy = 2 - 4 * (self.p // 2)
        self.chip = (self.p, self.p + dx, self.p + dy, self.p + dx + dy)
        self.core = 1 - self.c
        self.open, self.first = [], {}

    def dev(self, chip, core):
        return {"fsdp": 2 * chip + core}

    def rep(self, d):
        return lax.rem(self.z + d, 4)

    def push(self, src, dst, ss, rs, dev, keep=True):
        cp = pltpu.make_async_remote_copy(src, dst, ss, rs, device_id=dev, device_id_type=MESH)
        cp.start()
        if keep:
            self.open.append(cp)
        return cp

    def arrive(self, dst, ss, rs, dev):
        pltpu.make_async_remote_copy(dst, dst, ss, rs, device_id=dev, device_id_type=MESH).wait_recv()

    def barrier(self):
        bar = pltpu.get_barrier_semaphore()
        for dev in self.peers():
            pl.semaphore_signal(bar, inc=1, device_id=dev, device_id_type=MESH)
        pl.semaphore_wait(bar, 7)

    def peers(self):
        out = [self.dev(self.p, self.core)]
        out += [self.dev(self.chip[k], self.c) for k in (1, 2, 3)]
        out += [{"rep": self.rep(d)} for d in (1, 2, 3)]
        return out

    def slot(self, i, f):
        R = self.R
        if i == 0:
            return R.gat.at[f]
        l, k = (i - 1) // 4, (i - 1) % 4
        ref = (R.wqkv, R.wo, R.wup, R.wd)[k]
        n = ref.shape[1] // 8
        return ref.at[l, pl.ds(pl.multiple_of(f * n, n), n)]

    def source(self, i):
        R = self.R
        if i == 0:
            return R.mine
        l, k = (i - 1) // 4, (i - 1) % 4
        return (R.sqkv, R.so, R.sup, R.sd)[k].at[l]

    def gather_start(self, i):
        R, src, dst = self.R, self.source(i), self.slot(i, self.f)
        self.push(src, dst, R.ags.at[i, 1], R.agr.at[i, 1], self.dev(self.chip[1], self.c))
        self.push(src, dst, R.ags.at[i, 2], R.agr.at[i, 2], self.dev(self.chip[2], self.c))
        self.push(src, dst, R.ags.at[i, 3], R.agr.at[i, 3], self.dev(self.chip[3], self.c))
        self.push(src, dst, R.ags.at[i, 0], R.agr.at[i, 0], self.dev(self.p, self.core))
        pltpu.make_async_copy(src, dst, R.loc.at[i]).start()

    def gather_forward(self, i):
        R = self.R
        for k in (1, 2, 3):
            own = self.slot(i, 2 * self.chip[k] + self.c)
            self.arrive(own, R.ags.at[i, k], R.agr.at[i, k], self.dev(self.chip[k], self.c))
            self.push(own, own, R.ags.at[i, 3 + k], R.agr.at[i, 3 + k], self.dev(self.p, self.core))

    def gather_finish(self, i):
        R = self.R
        pltpu.make_async_copy(self.source(i), self.slot(i, self.f), R.loc.at[i]).wait()
        for k in (0, 1, 2, 3):
            j = 0 if k == 0 else 3 + k
            dst = self.slot(i, 2 * self.chip[k] + self.core)
            self.arrive(dst, R.ags.at[i, j], R.agr.at[i, j], self.dev(self.p, self.core))

    def grads(self, t):
        R, l = self.R, t // 3
        d, p, x = ((R.dD, R.pD, R.xD), (R.dU, R.pU, R.xU), (R.dA, R.pA, R.xA))[t % 3]
        return d, p.at[l], x.at[l]

    def step1(self, t):
        R = self.R
        d, p, x = self.grads(t)
        self.first[t] = self.push(d.at[self.core], p, R.s1s.at[t], R.s1r.at[t], self.dev(self.p, self.core), False)

    def step2(self, t):
        R = self.R
        d, p, x = self.grads(t)
        self.first[t].wait()
        for k in (3, 1, 2, 0):
            ch = self.chip[k]
            p[ch] = (d[self.c, ch].astype(F32) + p[ch].astype(F32)).astype(BF16)
            if k:
                self.push(p.at[ch], x.at[k - 1], R.s2s.at[t, k - 1], R.s2r.at[t, k - 1], self.dev(ch, self.c))

    def step3(self, t):
        R = self.R
        d, p, x = self.grads(t)
        for k in (1, 2, 3):
            self.arrive(x.at[k - 1], R.s2s.at[t, k - 1], R.s2r.at[t, k - 1], self.dev(self.chip[k], self.c))
        s = R.zb.shape[2]
        w = R.zb.shape[3]
        for j in range(4):
            at = (slice(s * j, s * j + s), slice(None)) if t % 3 == 0 else (slice(None), slice(w * j, w * j + w))
            tot = p[(self.p, *at)].astype(F32)
            for k in range(3):
                tot = tot + x[(k, *at)].astype(F32)
            R.zb[t, j] = tot.astype(BF16)
        for e in (1, 2, 3):
            r = self.rep(e)
            self.push(R.zb.at[t, r], R.zr.at[t, self.z], R.s3s.at[t, e - 1], R.s3r.at[t, e - 1], {"rep": r})

    def step4(self, t):
        R = self.R
        tot = R.zb[t, self.z].astype(F32)
        for e in (1, 2, 3):
            r = self.rep(4 - e)
            self.arrive(R.zr.at[t, r], R.s3s.at[t, e - 1], R.s3r.at[t, e - 1], {"rep": r})
            tot = tot + R.zr[t, r].astype(F32)
        R.zout[t, self.z] = tot.astype(BF16)
        for e in (1, 2, 3):
            here = R.zout.at[t, self.z]
            self.push(here, here, R.s4s.at[t, e - 1], R.s4r.at[t, e - 1], {"rep": self.rep(e)})

    def step5(self, t):
        R = self.R
        for e in (1, 2, 3):
            r = self.rep(4 - e)
            self.arrive(R.zout.at[t, r], R.s4s.at[t, e - 1], R.s4r.at[t, e - 1], {"rep": r})

    def vec1(self, l):
        R = self.R
        R.v0[l] = jnp.sum(R.vacc[12 * l : 12 * l + 12], axis=1)
        self.push(R.v0.at[l], R.v1.at[l], R.s1s.at[6 + l], R.s1r.at[6 + l], self.dev(self.p, self.core))

    def vec2(self, l):
        R, t = self.R, 6 + l
        self.arrive(R.v1.at[l], R.s1s.at[t], R.s1r.at[t], self.dev(self.p, self.core))
        R.v2[l] = R.v0[l] + R.v1[l]
        for k in (1, 2, 3):
            self.push(R.v2.at[l], R.v3.at[l, k - 1], R.s2s.at[t, k - 1], R.s2r.at[t, k - 1], self.dev(self.chip[k], self.c))

    def vec3(self, l):
        R, t = self.R, 6 + l
        tot = R.v2[l]
        for k in (1, 2, 3):
            self.arrive(R.v3.at[l, k - 1], R.s2s.at[t, k - 1], R.s2r.at[t, k - 1], self.dev(self.chip[k], self.c))
            tot = tot + R.v3[l, k - 1]
        R.v4[l, self.z] = tot
        for e in (1, 2, 3):
            here = R.v4.at[l, self.z]
            self.push(here, here, R.s3s.at[t, e - 1], R.s3r.at[t, e - 1], {"rep": self.rep(e)})

    def vec4(self, l):
        R, t = self.R, 6 + l
        for e in (1, 2, 3):
            r = self.rep(4 - e)
            self.arrive(R.v4.at[l, r], R.s3s.at[t, e - 1], R.s3r.at[t, e - 1], {"rep": r})
        R.vout[12 * l : 12 * l + 12, :] = (R.v4[l, 0] + R.v4[l, 1]) + (R.v4[l, 2] + R.v4[l, 3])

    def place_vectors(self):
        R = self.R
        R.pk[...] = jnp.zeros(R.pk.shape, F32)
        n = R.small[0].shape[1]
        for l in range(2):
            for k, ref in enumerate(R.small[:8]):
                R.pk[12 * l + k : 12 * l + k + 1, :n] = ref[l : l + 1, :].astype(F32)
        row = lax.broadcasted_iota(jnp.int32, (128, 384), 0)
        col = lax.broadcasted_iota(jnp.int32, (128, 384), 1)
        put = (col == row + n * self.f) & (row < n)
        R.mine[...] = nn(R.pk[...].astype(BF16), put.astype(F32).astype(BF16))
        ub = R.small[8]
        w = ub.shape[1]
        row = lax.broadcasted_iota(jnp.int32, (w, 384), 0)
        col = lax.broadcasted_iota(jnp.int32, (w, 384), 1)
        put = (col == row + w * lax.rem(self.f, 2)).astype(F32).astype(BF16)
        moved = nn(ub[...], put)
        for l in range(2):
            for h in range(4):
                R.mine[12 * l + 8 + h : 12 * l + 9 + h, :] = moved[l : l + 1, :] * (self.p == h).astype(F32)


def single_kernel(names, *refs):
    R = NS(**dict(zip(names, refs)))
    R.rows = R.x.shape[0]
    R.datt, R.g = R.att, R.gin
    R.grad = lambda k, l: (R.dD, R.dU, R.dA)[k].at[l]
    compute(R, (R.x, R.mid, R.out), lambda *a: None)
    R.vg[...] = jnp.sum(R.vacc[...], axis=1)


def single(x, cot, seg, vec, wqkv, wo, wup, wd):
    (rows, d), f = x.shape, wd.shape[1]
    sc = scratch_single(rows, d, f)
    names = ("x", "cot", "seg", "vec", "wqkv", "wo", "wup", "wd", "out", "gin", "dA", "dU", "dD", "vg", *sc)
    s = jax.ShapeDtypeStruct
    return pl.pallas_call(
        functools.partial(single_kernel, names),
        out_shape=(
            s((rows, d), F32), s((rows, d), F32), s((2, 2, 4, d // 8, f), BF16), s((2, 2, 4, d // 8, f), BF16),
            s((2, 2, 4, f // 8, d), BF16), s((24, d), F32)),
        in_specs=[pl.BlockSpec(memory_space=pltpu.VMEM)] * 8,
        out_specs=[pl.BlockSpec(memory_space=pltpu.VMEM)] * 6,
        scratch_shapes=list(sc.values()),
        compiler_params=pltpu.CompilerParams(vmem_limit_bytes=67043328),
    )(x, cot, seg, vec, wqkv, wo, wup, wd)


def fused_kernel(names, *refs):
    R = NS(**dict(zip(names, refs)))
    R.small = [getattr(R, "p%d" % i) for i in range(9)]
    R.rows = R.xb.shape[0]
    R.datt, R.g = R.att, R.mid
    R.grad = lambda k, l: (R.dD, R.dU, R.dA)[k]
    load = pltpu.make_async_copy(R.x, R.xb, R.io.at[0])
    load.start()
    C = Comm(R)
    C.place_vectors()
    C.barrier()
    for i in range(9):
        C.gather_start(i)
    load.wait()

    def hook(name, l):
        t = 3 * l
        if name == "qkv":
            if l == 0:
                C.gather_forward(0)
            C.gather_forward(1 + 4 * l)
            if l == 0:
                C.gather_finish(0)
                R.vec[...] = jnp.sum(R.gat[...], axis=0)
            C.gather_finish(1 + 4 * l)
        if name == "att":
            C.gather_forward(2 + 4 * l)
        if name == "mlp":
            C.gather_forward(3 + 4 * l)
            C.gather_forward(4 + 4 * l)
            for k in (2, 3, 4):
                C.gather_finish(k + 4 * l)
        if name == "fwd":
            pltpu.make_async_copy(R.xb, R.out, R.io.at[1]).start()
        if name == "b0" and l == 0:
            C.step3(5)
            C.vec2(1)
        if name == "dD":
            C.step1(t)
            if l == 0:
                C.step4(5)
                C.vec3(1)
        if name == "dU":
            C.step2(t)
            C.step1(t + 1)
        if name == "batt":
            C.step2(t + 1)
            C.step3(t)
        if name == "dA":
            C.step1(t + 2)
            C.step3(t + 1)
            C.step4(t)
        if name == "b1":
            C.vec1(l)
            C.step2(t + 2)
            C.step4(t + 1)

    compute(R, (R.xb, R.mid, R.xb), hook)
    save = pltpu.make_async_copy(R.g, R.gin, R.io.at[2])
    save.start()
    C.vec2(0)
    C.step3(2)
    C.vec3(0)
    C.step4(2)
    C.vec4(1)
    C.vec4(0)
    for t in (3, 4, 5, 0, 1, 2):
        C.step5(t)
    for cp in C.open:
        cp.wait_send()
    pltpu.make_async_copy(R.xb, R.out, R.io.at[1]).wait()
    save.wait()


def fused(x, cot, seg, small, sqkv, so, sup, sd):
    (rows, d), f = x.shape, 8 * sd.shape[1]
    sc = dict(xb=pltpu.VMEM((rows, d), F32), io=pltpu.SemaphoreType.DMA((3,)), **scratch_single(rows, d, f), **scratch_comm(d, f))
    ins = ("x", "cot", "seg", *("p%d" % i for i in range(9)), "sqkv", "so", "sup", "sd")
    names = (*ins, "out", "gin", "zout", "vout", *sc)
    s = jax.ShapeDtypeStruct
    any_, vm = pl.BlockSpec(memory_space=pl.ANY), pl.BlockSpec(memory_space=pltpu.VMEM)
    return pl.pallas_call(
        functools.partial(fused_kernel, names),
        out_shape=(s((rows, d), F32), s((rows, d), F32), s((6, 4, d // 8, d), BF16), s((24, d), F32)),
        in_specs=[any_] + [vm] * 11 + [any_] * 4,
        out_specs=[any_, any_, vm, vm],
        scratch_shapes=list(sc.values()),
        compiler_params=pltpu.CompilerParams(vmem_limit_bytes=67043328, collective_id=0, has_side_effects=True),
    )(x, cot, seg, *small, sqkv, so, sup, sd)


def finish_kernel(*refs):
    out, gin, zout, vout = refs[:4]
    o_out, o_gin, n1g, n1b, qkv, qb, vb, wo, ob, n2g, n2b, up, ub, down, db, buf, sem = refs[4:]
    loads = [pltpu.make_async_copy(src, buf.at[i], sem.at[i]) for i, src in enumerate((out, gin))]
    saves = [pltpu.make_async_copy(buf.at[i], dst, sem.at[i + 2]) for i, dst in enumerate((o_out, o_gin))]
    for cp in loads:
        cp.start()
    f = lax.axis_index("fsdp")
    s, w = zout.shape[2:]
    for l in range(2):
        for j in range(4):
            if j < 3:
                qkv[l, :, w * j : w * j + w] = zout[3 * l + 2, j].astype(F32)
            else:
                wo[l] = zout[3 * l + 2, j].astype(F32)
            up[l, :, w * j : w * j + w] = zout[3 * l + 1, j].astype(F32)
            down[l, s * j : s * j + s, :] = zout[3 * l, j].astype(F32)
    v = pltpu.roll(vout[...], lax.rem(w - s * f, w), 1)
    u = vout[8:12, :]
    half = 4 * s * lax.rem(f, 2)
    for l in range(2):
        for k, ref in enumerate((n1g, n1b, qb, vb, ob, n2g, n2b, db)):
            ref[l : l + 1, :] = v[12 * l + k : 12 * l + k + 1, :s]
        row = vout[pl.ds(12 * l + 8 + f // 2, 1), :]
        ub[l : l + 1, :] = pltpu.roll(jnp.broadcast_to(row, (8, w)), lax.rem(w - half, w), 1)[:1, : 4 * s]
    for a, b in zip(loads, saves):
        a.wait()
        b.start()
    for b in saves:
        b.wait()


def finish(out, gin, zout, vout):
    rows, d = out.shape
    s = d // 8
    t = jax.ShapeDtypeStruct
    vec = t((2, s), F32)
    any_, vm = pl.BlockSpec(memory_space=pl.ANY), pl.BlockSpec(memory_space=pltpu.VMEM)
    return pl.pallas_call(
        finish_kernel,
        out_shape=(
            t((rows, d), F32), t((rows, d), F32), vec, vec, t((2, s, 3 * d), F32), vec, vec, t((2, s, d), F32), vec, vec, vec,
            t((2, s, 4 * d), F32), t((2, 4 * s), F32), t((2, 4 * s, d), F32), vec),
        in_specs=[any_, any_, vm, vm],
        out_specs=[any_, any_] + [vm] * 13,
        scratch_shapes=[pltpu.VMEM((2, rows, d), F32), pltpu.SemaphoreType.DMA((4,))],
    )(out, gin, zout, vout)


def local_fused(x, cot, seg, n1g, n1b, qkv, qb, vb, wo, ob, n2g, n2b, up, ub, down, db):
    small = (n1g, n1b, qb, vb, ob, n2g, n2b, db, ub)
    return finish(*fused(x, cot, seg[None], small, qkv, wo, up, down))


def local_plain(x, cot, seg, n1g, n1b, qkv, qb, vb, wo, ob, n2g, n2b, up, ub, down, db):
    def gather(a):
        return lax.all_gather(a, "fsdp", axis=1, tiled=True)

    def scatter(a):
        return lax.psum(lax.psum_scatter(a, "fsdp", scatter_dimension=1, tiled=True), "rep")

    d = x.shape[1]
    vecs = jnp.stack([gather(a) for a in (n1g, n1b, qb, vb, ob, n2g, n2b, db)], 1)
    vec = jnp.concatenate([vecs, gather(ub).reshape(2, 4, d)], 1).astype(F32).reshape(24, d)
    out, gin, da, du, dd, vg = single(x, cot, seg[None], vec, gather(qkv), gather(wo), gather(up), gather(down))
    da, du, dd = (jnp.swapaxes(a, 1, 2).reshape(2, -1, a.shape[-1]).astype(F32) for a in (da, du, dd))
    da, du, dd = scatter(da), scatter(du), scatter(dd)
    vg = vg.reshape(2, 12, d)
    g = [scatter(vg[:, k]) for k in range(8)]
    gub = scatter(vg[:, 8:].reshape(2, 4 * d))
    return (out, gin, g[0], g[1], da[..., : 3 * d], g[2], g[3], da[..., 3 * d :], g[4], g[5], g[6], du, gub, dd, g[7])


def solution(mesh):
    from jax.sharding import PartitionSpec as P

    vec, mat, row = P(None, "fsdp"), P(None, "fsdp", None), P(("rep", "fsdp"), None)
    params = (vec, vec, mat, vec, vec, mat, vec, vec, vec, mat, vec, mat, vec)
    local = local_fused if dict(mesh.shape) == {"rep": 4, "fsdp": 8} else local_plain
    return jax.shard_map(local, mesh=mesh, in_specs=(row, row, P(("rep", "fsdp")), *params), out_specs=(row, row, *params), check_vma=False)
```

time: 1010 us -> 170 us (0.17)
  waiting for transfers between devices: 502 us -> 0 us
  matrix products: 199 us -> 0 us
  Pallas kernels: 0 us -> 169 us
  local copies, waits for them, and re-layouts: 101 us -> 0 us
  other arithmetic: 94.8 us -> 0 us
  blocking collectives: 88.6 us -> 0 us
  between operations: 18 us -> 0.82 us
    unnamed x27 -> x0, waiting for transfers between devices: 313 us -> none
    dot_general x48 -> x0, matrix products: 199 us -> none  [the longest x24 77.2 us: matmul(): return jnp.dot(left, right, preferred_element_type=jnp.float32)]
    pallas_call x0 -> x2, Pallas kernels: none -> 169 us  [the longest x1 163 us: fused(): pl.pallas_call(functools.partial(fused_kernel, names), out_shape=(s((rows...]
    reduce_scatter x4 -> x0, waiting for transfers between devices: 132 us -> none  [the longest x1 57.2 us: local(): lax.psum_scatter(stacked[9], 'fsdp', scatter_dimension=1, tiled=True)]
    psum x1 -> x0, waiting for transfers between devices: 57.1 us -> none  [local(): lax.psum((shard_sums[0], shard_sums[1], shard_sums[2], shard_sums[3], sha...]
    unnamed x387 -> x0, local copies, waits for them, and re-layouts: 55.7 us -> none
    convert_element_type x24 -> x0, other arithmetic: 46.9 us -> none  [the longest x3 36.8 us: attend_backward(): grad_scores = (probs * (grad_probs - delta)).astype(jnp.bfloat16)]
    all_gather x4 -> x0, blocking collectives: 42 us -> none  [the longest x2 21.7 us: fetch_forward(): lax.all_gather(shards[2][layer_idx], 'fsdp', axis=0, tiled=True)]
  transfers between devices with their start and end apart: 18 -> 0, of which waited for: 13 -> 0; matrix products, arithmetic and copies ran while one was open for 20% -> 0% of each run, Pallas kernels for 0% -> 0%
where the time goes in v1:
time: 170 us; the launch traced here: 169 us
  Pallas kernels  169 us (99%)
    pallas_call x1, Pallas kernels, fused(): pl.pallas_call(functools.partial(fused_kernel, names), out_shape=(s((rows...  163 us
    pallas_call x1, Pallas kernels, finish(): pl.pallas_call(finish_kernel, out_shape=(t((rows, d), F32), t((rows, d),...  5.55 us

profile of v1, /device:TPU:0, one launch (start us, length us, event | category | flops | bytes accessed | tf_op | source)
XLA Modules:
  0.0 169.4 jit_solution(9826575872250617923)
XLA Ops:
  0.7 163.0 %shard_map.271 = (f32[1024,384]{1,0:T(8,128)}, f32[1024,384]{1,0:T(8,128)}, bf16[6,4,48,384]{3,2,1,0:T(8,128)(2,1)}, f32[24,384]{1,0:T(8,128)}) custom-call(f32[1024,384]{1,0:T(8,128)} %refs_0_.1, f32[1024,384]{1,0:T(8,128)} %refs_1_.1, s32[1,1024]{1,0:T(1,128)} %bitcast.1, bf16[2,48]{1,0:T(2,128)(2,1)} %refs_3_.1, bf16[2,48]{1,0:T(2,128)(2,1)} %refs_4_.1, ...), custom_call_target="tpu_custom_call" | custom-call | tf_op jit(solution)/shard_map/pallas_call | solution.py:680
  163.6 5.5 %shard_map.272 = (f32[1024,384]{1,0:T(8,128)}, f32[1024,384]{1,0:T(8,128)}, f32[2,48]{1,0:T(2,128)}, f32[2,48]{1,0:T(2,128)}, f32[2,48,1152]{2,1,0:T(8,128)}, /*...) custom-call(f32[1024,384]{1,0:T(8,128)} %get-tuple-element.19.refs_0, ...), custom_call_target="tpu_custom_call" | custom-call | tf_op jit(solution)/shard_map/pallas_call | solution.py:728

commit v2 on v1

--- a/solution.py
+++ b/solution.py
@@ -9,15 +9,19 @@
 HEADS = 6
 HEAD_DIM = 64
 IMG = 197
-STEP = 192
-QWIN = 224
-KWIN = 256
 TILE = 256
 norm_eps = 1e-06
 neg_fill = -1e30
 root_half = 0.7071067811865476
 inv_root_tau = 0.3989422804014327
 F32, BF16 = jnp.float32, jnp.bfloat16
+LOG2E = 1.4426950408889634
+FORE = ((0, 256), (0, 448), (192, 448), (192, 1024), (384, 1024), (384, 1024), (384, 1024), (384, 1024))
+BACK = ((0, 208), (0, 400), (192, 400), (192, 592), (384, 800), (576, 800), (576, 992), (784, 992))
+BASE = tuple(sum(e - s for s, e in FORE[:b]) for b in range(9))
+FORE_ORDER = (4, 5, 3, 6, 7, 1, 2, 0)
+BACK_ORDER = (3, 4, 6, 1, 5, 0, 2, 7)
+SLOTS, SLOT = 3, 832
 
 
 def nn(a, b):
@@ -48,8 +52,8 @@
 
 
 def gelu_both(pre):
-    cdf = 0.5 * (1.0 + lax.erf(pre * root_half))
-    return pre * cdf, cdf + pre * jnp.exp(-0.5 * pre * pre) * inv_root_tau
+    cdf = 0.5 * lax.erf(pre * root_half) + 0.5
+    return pre * cdf, cdf + (pre * inv_root_tau) * jnp.exp2(pre * pre * (-0.5 * LOG2E))
 
 
 def vrow(R, l, k):
@@ -66,12 +70,12 @@
     def tile(i, c):
         rows = pl.ds(pl.multiple_of(i * TILE, TILE), TILE)
         n, r = norm(src[rows, :])
-        R.n1[l, rows, :] = n
+        R.n1[l, rows, :] = n.astype(BF16)
         R.stats[l, rows, 0:1] = r
         a = (n * gain + bias).astype(BF16)
         R.aT[l, :, rows] = a.T
         proj = nn(a, R.wqkv[l])
-        R.q[l, rows, :] = ((proj[:, :384] + qb) * (HEAD_DIM**-0.5)).astype(BF16)
+        R.q[l, rows, :] = ((proj[:, :384] + qb) * (HEAD_DIM**-0.5 * LOG2E)).astype(BF16)
         R.k[l, rows, :] = proj[:, 384:768].astype(BF16)
         R.v[l, rows, :] = (proj[:, 768:] + vb).astype(BF16)
         return c
@@ -84,88 +88,83 @@
     return jnp.concatenate([jnp.where(low, x, zero), jnp.where(low, zero, x)], 0)
 
 
-def attend(q, k, v, bias):
-    n = q.shape[0]
-    low = lax.broadcasted_iota(jnp.int32, (1, 128), 1) < HEAD_DIM
-    s = nt(stack_heads(q, low), k)
-    if bias.shape[0] == n:
-        bias = jnp.concatenate([bias, bias], 0)
-    s = s + bias
-    top = jnp.max(s, -1, keepdims=True)
-    p = jnp.exp(s - top)
-    den = jnp.sum(p, -1, keepdims=True)
-    o = nn((p * (1.0 / den)).astype(BF16), v)
-    return jnp.where(low, o[:n], o[n:]).astype(BF16), top + jnp.log(den)
-
+def lowlanes():
+    return lax.broadcasted_iota(jnp.int32, (1, 128), 1) < HEAD_DIM
+
+def twice(x):
+    return jnp.concatenate([x, x], 1)
 
 def stage_attend(R, l):
-    def put(pr, start, first, o, lse):
-        n = o.shape[0]
-        lanes = slice(128 * pr, 128 * pr + 128)
-        head = pl.ds(start, 32)
-        rest = pl.ds(start + 32, n - 32)
-        old = start + lax.broadcasted_iota(jnp.int32, (32, 1), 0) < first
-        R.att[head, lanes] = jnp.where(old, R.att[head, lanes].astype(F32), o[:32].astype(F32)).astype(BF16)
-        R.att[rest, lanes] = o[32:]
-        for h in range(2):
-            col = slice(2 + 2 * pr + h, 3 + 2 * pr + h)
-            R.stats[l, head, col] = jnp.where(old, R.stats[l, head, col], lse[n * h : n * h + 32])
-            R.stats[l, rest, col] = lse[n * h + 32 : n * h + n]
-
-    def window(j, c):
-        start = pl.multiple_of(j * STEP, STEP)
-        col = lax.broadcasted_iota(jnp.int32, (1, KWIN), 1)
-        bias = jnp.where((col >= 5 * j) & (col < 5 * j + IMG), 0.0, neg_fill)
-        for pr in range(3):
-            lanes = slice(128 * pr, 128 * pr + 128)
-            o, lse = attend(
-                R.q[l, pl.ds(start, QWIN), lanes], R.k[l, pl.ds(start, KWIN), lanes],
-                R.v[l, pl.ds(start, KWIN), lanes], bias)
-            put(pr, start, IMG * j, o, lse)
-        return c
-
-    lax.fori_loop(0, 2, window, 0)
-
-    def rest(t, c):
-        start = pl.multiple_of(2 * STEP + t * 128, 128)
-        bias = R.segbias[pl.ds(pl.multiple_of(t * 128, 128), 128), :]
-        for pr in range(3):
-            lanes = slice(128 * pr, 128 * pr + 128)
-            o, lse = attend(
-                R.q[l, pl.ds(start, 128), lanes], R.k[l, 2 * STEP :, lanes],
-                R.v[l, 2 * STEP :, lanes], bias)
-            put(pr, start, 2 * IMG, o, lse)
-        return c
-
-    lax.fori_loop(0, (R.rows - 2 * STEP) // 128, rest, 0)
-
+    low = lowlanes()
+
+    def pair(pr, c):
+        lanes = pl.ds(pl.multiple_of(pr * 128, 128), 128)
+
+        def scores(i, b):
+            s, e = FORE[b]
+            q = stack_heads(R.q[l, 128 * b : 128 * b + 128, lanes], low)
+            R.fb[i % SLOTS, : e - s, :] = nt(R.k[l, s:e, lanes], q)
+
+        def finish(i, b):
+            s, e = FORE[b]
+            x = R.fb[i % SLOTS, : e - s, :] + twice(R.bias[BASE[b] : BASE[b + 1], :])
+            top = jnp.max(x, 0, keepdims=True)
+            p = jnp.exp2(x - top)
+            den = jnp.sum(p, 0, keepdims=True)
+            p = p.astype(BF16)
+            vt = R.v[l, s:e, lanes].T
+            inv = 1.0 / den
+            o = jnp.concatenate([nn(vt[:64], p[:, :128]) * inv[:, :128], nn(vt[64:], p[:, 128:]) * inv[:, 128:]], 0)
+            R.att[128 * b : 128 * b + 128, lanes] = o.T.astype(BF16)
+            e = top + jnp.log2(den)
+            R.lse[l, pr, 0:1, 128 * b : 128 * b + 128] = e[:, :128]
+            R.lse[l, pr, 1:2, 128 * b : 128 * b + 128] = e[:, 128:]
+
+        order = FORE_ORDER
+        for i, b in enumerate(order):
+            scores(i, b)
+            if i >= SLOTS - 1:
+                finish(i - SLOTS + 1, order[i - SLOTS + 1])
+        for i in range(len(order) - SLOTS + 1, len(order)):
+            finish(i, order[i])
+        return c
+
+    lax.fori_loop(0, 3, pair, 0)
 
 def stage_mlp(R, l, src, dst):
     ob, gain, bias, db = (vrow(R, l, k) for k in (4, 5, 6, 7))
-
-    def tile(i, c):
-        rows = pl.ds(pl.multiple_of(i * TILE, TILE), TILE)
+    ub = jnp.concatenate([vrow(R, l, 8 + ch) for ch in range(4)], 1)
+    last = R.rows // TILE - 1
+
+    def project(rows):
         att = R.att[rows, :]
         R.attT[l, :, rows] = att.T
-        mid = src[rows, :] + nn(att, R.wo[l]) + ob
+        return src[rows, :] + nn(att, R.wo[l]) + ob
+
+    def prepare(rows, mid):
         n, r = norm(mid)
-        R.n2[l, rows, :] = n
+        R.n2[l, rows, :] = n.astype(BF16)
         R.stats[l, rows, 1:2] = r
         m = (n * gain + bias).astype(BF16)
         R.mT[l, :, rows] = m.T
-        acc = mid + db
-        for ch in range(4):
-            cols = slice(384 * ch, 384 * ch + 384)
-            pre = nn(m, R.wup[l, :, cols]) + vrow(R, l, 8 + ch)
-            hid, slope = gelu_both(pre)
-            hid = hid.astype(BF16)
-            R.hidT[l, cols, rows] = hid.T
-            R.slope[l, rows, cols] = slope.astype(BF16)
-            acc = acc + nn(hid, R.wd[l, cols, :])
-        dst[rows, :] = acc
-        return c
-
-    lax.fori_loop(0, R.rows // TILE, tile, 0)
+        R.gml[:TILE, :] = m
+        R.midb[...] = mid + db
+
+    def tile(i, c):
+        rows = pl.ds(pl.multiple_of(i * TILE, TILE), TILE)
+        after = pl.ds(pl.multiple_of(jnp.minimum(i + 1, last) * TILE, TILE), TILE)
+        base = R.midb[...]
+        hid, slope = gelu_both(nn(R.gml[:TILE, :], R.wup[l]) + ub)
+        hid = hid.astype(BF16)
+        R.slope[l, rows, :] = slope.astype(BF16)
+        prepare(after, project(after))
+        dst[rows, :] = base + nn(hid, R.wd[l])
+        R.hidT[l, :, rows] = hid.T
+        return c
+
+    start = pl.ds(0, TILE)
+    prepare(start, project(start))
+    lax.fori_loop(0, last + 1, tile, 0)
 
 
 def stage_mlp_back(R, l):
@@ -174,8 +173,7 @@
     def tile(i, c):
         rows = pl.ds(pl.multiple_of(i * TILE, TILE), TILE)
         g = R.g[rows, :]
-        gl = g.astype(BF16)
-        R.gl[rows, :] = gl
+        gl = R.gl[rows, :]
         add_sum(R, l, 7, g)
         dm = jnp.zeros_like(g)
         for ch in range(4):
@@ -185,7 +183,7 @@
             dpre = dpre.astype(BF16)
             R.slope[l, rows, cols] = dpre
             dm = dm + nt(dpre, R.wup[l, :, cols])
-        n = R.n2[l, rows, :]
+        n = R.n2[l, rows, :].astype(F32)
         add_sum(R, l, 5, dm * n)
         add_sum(R, l, 6, dm)
         gm = g + norm_back(dm, n, R.stats[l, rows, 1:2], gain)
@@ -238,47 +236,52 @@
 
 
 def stage_attend_back(R, l):
-    R.dproj[...] = jnp.zeros(R.dproj.shape, BF16)
-    low = lax.broadcasted_iota(jnp.int32, (1, 128), 1) < HEAD_DIM
-
-    def put(start, col, x):
-        n = x.shape[0]
-        head = pl.ds(start, 32)
-        lanes = slice(col, col + 128)
-        R.dproj[head, lanes] = (R.dproj[head, lanes].astype(F32) + x[:32]).astype(BF16)
-        R.dproj[pl.ds(start + 32, n - 32), lanes] = x[32:].astype(BF16)
-
-    def window(j, c):
-        start = pl.multiple_of(j * STEP, STEP)
-        qrows, krows = pl.ds(start, QWIN), pl.ds(start, KWIN)
-        col = lax.broadcasted_iota(jnp.int32, (1, KWIN), 1)
-        colbias = jnp.where((col >= 5 * j) & (col < 5 * j + IMG), 0.0, neg_fill)
-        row = lax.broadcasted_iota(jnp.int32, (QWIN, 1), 0)
-        rowin = (row >= 5 * j) & (row < 5 * j + IMG)
-        for pr in range(3):
-            lanes = slice(128 * pr, 128 * pr + 128)
-            q01 = stack_heads(R.q[l, qrows, lanes], low)
-            do01 = stack_heads(R.datt[qrows, lanes], low)
-            k, v = R.k[l, krows, lanes], R.v[l, krows, lanes]
-            lse01 = jnp.concatenate(
-                [jnp.where(rowin, R.stats[l, qrows, c : c + 1], -neg_fill) for c in (2 + 2 * pr, 3 + 2 * pr)], 0)
-            p = jnp.exp((nt(q01, k) - lse01) + colbias)
-            pdp = nt(do01, v)
-            delta = jnp.sum(p * pdp, -1, keepdims=True)
-            ds = (p * (pdp - delta)).astype(BF16)
-            dq01 = nn(ds, k)
-            dq = jnp.where(low, dq01[:QWIN], dq01[QWIN:]) * (HEAD_DIM**-0.5)
-            dk = tn(ds, q01)[:QWIN]
-            dv = tn(p.astype(BF16), do01)[:QWIN]
-            put(start, 128 * pr, dq)
-            put(start, 384 + 128 * pr, dk)
-            put(start, 768 + 128 * pr, dv)
+    low = lowlanes()
+
+    def pair(pr, c):
+        off = pl.multiple_of(pr * 128, 128)
+        lanes = pl.ds(off, 128)
+        R.dk[...] = jnp.zeros((R.rows, 128), F32)
+        R.dv[...] = jnp.zeros((R.rows, 128), F32)
+
+        def scores(i, b):
+            s, e = BACK[b]
+            rows = slice(128 * b, 128 * b + 128)
+            R.fb[i % SLOTS, : e - s, :] = nt(R.k[l, s:e, lanes], stack_heads(R.q[l, rows, lanes], low))
+            R.fb[i % SLOTS, 416 : 416 + e - s, :] = nt(R.v[l, s:e, lanes], stack_heads(R.datt[rows, lanes], low))
+
+        def finish(i, b):
+            s, e = BACK[b]
+            rows = slice(128 * b, 128 * b + 128)
+            base = BASE[b] + s - FORE[b][0]
+            lse = jnp.concatenate([R.lse[l, pr, 0:1, rows], R.lse[l, pr, 1:2, rows]], 1)
+            x = R.fb[i % SLOTS, : e - s, :] + twice(R.bias[base : base + e - s, :])
+            p = jnp.exp2(x - lse)
+            dp = R.fb[i % SLOTS, 416 : 416 + e - s, :]
+            delta = jnp.sum(p * dp, 0, keepdims=True)
+            ds = (p * (dp - delta)).astype(BF16)
+            p = p.astype(BF16)
+            R.dv[s:e, :] += nn(p, stack_heads(R.datt[rows, lanes], low))
+            R.dk[s:e, :] += nn(ds, stack_heads(R.q[l, rows, lanes], low))
+            kt = R.k[l, s:e, lanes].T
+            dq = jnp.concatenate([nn(kt[:64], ds[:, :128]), nn(kt[64:], ds[:, 128:])], 0).T * (HEAD_DIM**-0.5)
             R.vacc[12 * l + 2, :, lanes] += fold8(dq)
-            R.vacc[12 * l + 3, :, lanes] += fold8(dv)
-        return c
-
-    lax.fori_loop(0, 5, window, 0)
-
+            R.dproj[rows, lanes] = dq.astype(BF16)
+
+        order = BACK_ORDER
+        for i, b in enumerate(order):
+            scores(i, b)
+            if i >= SLOTS - 1:
+                finish(i - SLOTS + 1, order[i - SLOTS + 1])
+        for i in range(len(order) - SLOTS + 1, len(order)):
+            finish(i, order[i])
+        dv = R.dv[...]
+        R.vacc[12 * l + 3, :, lanes] += fold8(dv)
+        R.dproj[:, pl.ds(384 + off, 128)] = (R.dk[...] * (1.0 / LOG2E)).astype(BF16)
+        R.dproj[:, pl.ds(768 + off, 128)] = dv.astype(BF16)
+        return c
+
+    lax.fori_loop(0, 3, pair, 0)
 
 def stage_qkv_back(R, l):
     gain = vrow(R, l, 0)
@@ -286,10 +289,13 @@
     def tile(i, c):
         rows = pl.ds(pl.multiple_of(i * TILE, TILE), TILE)
         da = nt(R.dproj[rows, :], R.wqkv[l])
-        n = R.n1[l, rows, :]
+        n = R.n1[l, rows, :].astype(F32)
         add_sum(R, l, 0, da * n)
         add_sum(R, l, 1, da)
-        R.g[rows, :] = R.g[rows, :] + norm_back(da, n, R.stats[l, rows, 0:1], gain)
+        g = R.g[rows, :] + norm_back(da, n, R.stats[l, rows, 0:1], gain)
+        R.g[rows, :] = g
+        if l:
+            R.gl[rows, :] = g.astype(BF16)
         return c
 
     lax.fori_loop(0, R.rows // TILE, tile, 0)
@@ -298,22 +304,18 @@
 def stage_segments(R):
     seg = R.seg[...].astype(F32)
     cols = jnp.broadcast_to(seg, (128, R.rows)).T
-    R.segcol[...] = cols
-    keys = seg[:, 2 * STEP :]
-
-    def tile(t, c):
-        rows = pl.ds(pl.multiple_of(t * 128, 128), 128)
-        mine = R.segcol[pl.ds(pl.multiple_of(2 * STEP + t * 128, 128), 128), :1]
-        R.segbias[rows, :] = jnp.where(mine == keys, 0.0, neg_fill)
-        return c
-
-    lax.fori_loop(0, (R.rows - 2 * STEP) // 128, tile, 0)
+    R.stats[0, :, 2:3] = cols[:, :1]
+    for b in range(8):
+        i, j = FORE[b]
+        R.bias[BASE[b] : BASE[b + 1], :] = jnp.where(cols[i:j] == seg[:, 128 * b : 128 * b + 128], 0.0, neg_fill)
 
 
 def stage_cotangent(R):
     def tile(i, c):
         rows = pl.ds(pl.multiple_of(i * TILE, TILE), TILE)
-        R.g[rows, :] = jnp.where(R.segcol[rows, :1] >= 0.0, R.cot[rows, :], 0.0)
+        g = jnp.where(R.stats[0, rows, 2:3] >= 0.0, R.cot[rows, :], 0.0)
+        R.g[rows, :] = g
+        R.gl[rows, :] = g.astype(BF16)
         return c
 
     lax.fori_loop(0, R.rows // TILE, tile, 0)
@@ -332,10 +334,10 @@
     hook("fwd", 0)
     stage_cotangent(R)
     for l in (1, 0):
+        stage_weight_down(R, l)
+        hook("dD", l)
         stage_mlp_back(R, l)
         hook("b0", l)
-        stage_weight_down(R, l)
-        hook("dD", l)
         stage_weight_up(R, l)
         hook("dU", l)
         stage_weight_out(R, l)
@@ -355,12 +357,13 @@
 def scratch_single(rows, d, f):
     v = pltpu.VMEM
     return dict(
-        mid=v((rows, d), F32), n1=v((2, rows, d), F32), n2=v((2, rows, d), F32),
+        mid=v((rows, d), F32), n1=v((2, rows, d), BF16), n2=v((2, rows, d), BF16),
         stats=v((2, rows, 128), F32), aT=v((2, d, rows), BF16),
         q=v((2, rows, d), BF16), k=v((2, rows, d), BF16), v=v((2, rows, d), BF16),
         att=v((rows, d), BF16), attT=v((2, d, rows), BF16), mT=v((2, d, rows), BF16),
         hidT=v((2, f, rows), BF16), slope=v((2, rows, f), BF16),
-        segcol=v((rows, 128), F32), segbias=v((rows - 2 * STEP, rows - 2 * STEP), F32),
+        bias=v((BASE[8], 128), F32), lse=v((2, 3, 2, rows), F32), fb=v((SLOTS, SLOT, 256), F32),
+        midb=v((TILE, d), F32),
         gl=v((rows, d), BF16), gml=v((rows, d), BF16),
         dproj=v((rows, 3 * d), BF16), vacc=v((24, 8, d), F32),
     )
@@ -375,10 +378,10 @@
         dD=v((2, 4, t, d), BF16), dU=v((2, 4, s, f), BF16), dA=v((2, 4, s, f), BF16),
         pD=v((2, 4, t, d), BF16), pU=v((2, 4, s, f), BF16), pA=v((2, 4, s, f), BF16),
         xD=v((2, 3, t, d), BF16), xU=v((2, 3, s, f), BF16), xA=v((2, 3, s, f), BF16),
-        zb=v((6, 4, s, d), BF16), zr=v((6, 4, s, d), BF16),
-        v0=v((2, 12, d), F32), v1=v((2, 12, d), F32), v2=v((2, 12, d), F32), v3=v((2, 3, 12, d), F32), v4=v((2, 4, 12, d), F32),
+        zb=v((6, 4, s, d), BF16), zr=v((6, 4, s, d), BF16), zs=v((6, s, d), BF16),
+        v0=v((2, 12, d), F32), v1=v((2, 12, d), F32), v2=v((2, 12, d), F32), v3=v((2, 3, 12, d), F32), v4=v((2, 4, 12, d), F32), vs=v((2, 12, d), F32), vl=dma((2,)),
         loc=dma((9,)), ags=dma((9, 7)), agr=dma((9, 7)), s1s=dma((8,)), s1r=dma((8,)), s2s=dma((8, 3)), s2r=dma((8, 3)),
-        s3s=dma((8, 3)), s3r=dma((8, 3)), s4s=dma((6, 3)), s4r=dma((6, 3)),
+        s3s=dma((8, 3)), s3r=dma((8, 3)), s4s=dma((6, 3)), s4r=dma((6, 3)), s4l=dma((6,)),
     )
 
 
@@ -507,16 +510,28 @@
             r = self.rep(4 - e)
             self.arrive(R.zr.at[t, r], R.s3s.at[t, e - 1], R.s3r.at[t, e - 1], {"rep": r})
             tot = tot + R.zr[t, r].astype(F32)
-        R.zout[t, self.z] = tot.astype(BF16)
+        R.zs[t] = tot.astype(BF16)
+        here = R.zout.at[t, self.z]
         for e in (1, 2, 3):
-            here = R.zout.at[t, self.z]
-            self.push(here, here, R.s4s.at[t, e - 1], R.s4r.at[t, e - 1], {"rep": self.rep(e)})
+            self.push(R.zs.at[t], here, R.s4s.at[t, e - 1], R.s4r.at[t, e - 1], {"rep": self.rep(e)})
+        pltpu.make_async_copy(R.zs.at[t], here, R.s4l.at[t]).start()
 
     def step5(self, t):
         R = self.R
         for e in (1, 2, 3):
             r = self.rep(4 - e)
             self.arrive(R.zout.at[t, r], R.s4s.at[t, e - 1], R.s4r.at[t, e - 1], {"rep": r})
+        pltpu.make_async_copy(R.zs.at[t], R.zout.at[t, self.z], R.s4l.at[t]).wait()
+
+    def late_sends(self):
+        for cp in self.open:
+            cp.wait_send()
+
+    def late_io(self, save):
+        pltpu.make_async_copy(self.R.xb, self.R.out, self.R.io.at[1]).wait()
+        save.wait()
+        for l in range(2):
+            pltpu.make_async_copy(self.R.vs.at[l], self.R.vout.at[l], self.R.vl.at[l]).wait()
 
     def vec1(self, l):
         R = self.R
@@ -546,7 +561,8 @@
         for e in (1, 2, 3):
             r = self.rep(4 - e)
             self.arrive(R.v4.at[l, r], R.s3s.at[t, e - 1], R.s3r.at[t, e - 1], {"rep": r})
-        R.vout[12 * l : 12 * l + 12, :] = (R.v4[l, 0] + R.v4[l, 1]) + (R.v4[l, 2] + R.v4[l, 3])
+        R.vs[l] = (R.v4[l, 0] + R.v4[l, 1]) + (R.v4[l, 2] + R.v4[l, 3])
+        pltpu.make_async_copy(R.vs.at[l], R.vout.at[l], R.vl.at[l]).start()
 
     def place_vectors(self):
         R = self.R
@@ -574,6 +590,7 @@
     R = NS(**dict(zip(names, refs)))
     R.rows = R.x.shape[0]
     R.datt, R.g = R.att, R.gin
+    R.dk, R.dv = R.dkv.at[0], R.dkv.at[1]
     R.grad = lambda k, l: (R.dD, R.dU, R.dA)[k].at[l]
     compute(R, (R.x, R.mid, R.out), lambda *a: None)
     R.vg[...] = jnp.sum(R.vacc[...], axis=1)
@@ -581,7 +598,7 @@
 
 def single(x, cot, seg, vec, wqkv, wo, wup, wd):
     (rows, d), f = x.shape, wd.shape[1]
-    sc = scratch_single(rows, d, f)
+    sc = dict(dkv=pltpu.VMEM((2, rows, 128), F32), **scratch_single(rows, d, f))
     names = ("x", "cot", "seg", "vec", "wqkv", "wo", "wup", "wd", "out", "gin", "dA", "dU", "dD", "vg", *sc)
     s = jax.ShapeDtypeStruct
     return pl.pallas_call(
@@ -596,14 +613,35 @@
     )(x, cot, seg, vec, wqkv, wo, wup, wd)
 
 
+PLAN = {
+    ("dD", 1): (("step1", 3),),
+    ("b0", 1): (("step2", 3),),
+    ("dU", 1): (("step1", 4),),
+    ("batt", 1): (("step2", 4), ("step3", 3)),
+    ("dA", 1): (("step1", 5),),
+    ("b1", 1): (("vec1", 1), ("step2", 5), ("step4", 3)),
+    ("dD", 0): (("step1", 0), ("step3", 4), ("vec2", 1)),
+    ("b0", 0): (("step2", 0), ("step3", 5), ("step4", 4), ("vec3", 1)),
+    ("dU", 0): (("step1", 1),),
+    ("dO", 0): (("step2", 1),),
+    ("batt", 0): (("step3", 0), ("step4", 5), ("vec4", 1)),
+    ("dA", 0): (("step1", 2),),
+    ("b1", 0): (("vec1", 0), ("step2", 2), ("step3", 1), ("step4", 0)),
+    ("tail", 0): (("vec2", 0), ("step3", 2), ("vec3", 0), ("step4", 1), ("step4", 2), ("vec4", 0)),
+}
+
+
 def fused_kernel(names, *refs):
     R = NS(**dict(zip(names, refs)))
     R.small = [getattr(R, "p%d" % i) for i in range(9)]
     R.rows = R.xb.shape[0]
     R.datt, R.g = R.att, R.mid
+    R.dk, R.dv = R.cot.at[:, :128], R.cot.at[:, 128:256]
     R.grad = lambda k, l: (R.dD, R.dU, R.dA)[k]
     load = pltpu.make_async_copy(R.x, R.xb, R.io.at[0])
     load.start()
+    cot = pltpu.make_async_copy(R.hcot, R.cot, R.io.at[3])
+    cot.start()
     C = Comm(R)
     C.place_vectors()
     C.barrier()
@@ -630,109 +668,94 @@
                 C.gather_finish(k + 4 * l)
         if name == "fwd":
             pltpu.make_async_copy(R.xb, R.out, R.io.at[1]).start()
-        if name == "b0" and l == 0:
-            C.step3(5)
-            C.vec2(1)
-        if name == "dD":
-            C.step1(t)
-            if l == 0:
-                C.step4(5)
-                C.vec3(1)
-        if name == "dU":
-            C.step2(t)
-            C.step1(t + 1)
-        if name == "batt":
-            C.step2(t + 1)
-            C.step3(t)
-        if name == "dA":
-            C.step1(t + 2)
-            C.step3(t + 1)
-            C.step4(t)
-        if name == "b1":
-            C.vec1(l)
-            C.step2(t + 2)
-            C.step4(t + 1)
+            cot.wait()
+        for what, k in PLAN.get((name, l), ()):
+            getattr(C, what)(k)
 
     compute(R, (R.xb, R.mid, R.xb), hook)
     save = pltpu.make_async_copy(R.g, R.gin, R.io.at[2])
     save.start()
-    C.vec2(0)
-    C.step3(2)
-    C.vec3(0)
-    C.step4(2)
-    C.vec4(1)
-    C.vec4(0)
+    for what, k in PLAN["tail", 0]:
+        getattr(C, what)(k)
     for t in (3, 4, 5, 0, 1, 2):
         C.step5(t)
-    for cp in C.open:
-        cp.wait_send()
-    pltpu.make_async_copy(R.xb, R.out, R.io.at[1]).wait()
-    save.wait()
+    C.late_sends()
+    C.late_io(save)
 
 
 def fused(x, cot, seg, small, sqkv, so, sup, sd):
     (rows, d), f = x.shape, 8 * sd.shape[1]
-    sc = dict(xb=pltpu.VMEM((rows, d), F32), io=pltpu.SemaphoreType.DMA((3,)), **scratch_single(rows, d, f), **scratch_comm(d, f))
-    ins = ("x", "cot", "seg", *("p%d" % i for i in range(9)), "sqkv", "so", "sup", "sd")
+    sc = dict(xb=pltpu.VMEM((rows, d), F32), cot=pltpu.VMEM((rows, d), F32), io=pltpu.SemaphoreType.DMA((4,)), **scratch_single(rows, d, f), **scratch_comm(d, f))
+    ins = ("x", "hcot", "seg", *("p%d" % i for i in range(9)), "sqkv", "so", "sup", "sd")
     names = (*ins, "out", "gin", "zout", "vout", *sc)
     s = jax.ShapeDtypeStruct
     any_, vm = pl.BlockSpec(memory_space=pl.ANY), pl.BlockSpec(memory_space=pltpu.VMEM)
     return pl.pallas_call(
         functools.partial(fused_kernel, names),
-        out_shape=(s((rows, d), F32), s((rows, d), F32), s((6, 4, d // 8, d), BF16), s((24, d), F32)),
-        in_specs=[any_] + [vm] * 11 + [any_] * 4,
-        out_specs=[any_, any_, vm, vm],
+        out_shape=(s((rows, d), F32), s((rows, d), F32), s((6, 4, d // 8, d), BF16), s((2, 12, d), F32)),
+        in_specs=[any_] * 2 + [vm] * 10 + [any_] * 4,
+        out_specs=[any_] * 4,
         scratch_shapes=list(sc.values()),
         compiler_params=pltpu.CompilerParams(vmem_limit_bytes=67043328, collective_id=0, has_side_effects=True),
     )(x, cot, seg, *small, sqkv, so, sup, sd)
 
 
 def finish_kernel(*refs):
-    out, gin, zout, vout = refs[:4]
-    o_out, o_gin, n1g, n1b, qkv, qb, vb, wo, ob, n2g, n2b, up, ub, down, db, buf, sem = refs[4:]
-    loads = [pltpu.make_async_copy(src, buf.at[i], sem.at[i]) for i, src in enumerate((out, gin))]
-    saves = [pltpu.make_async_copy(buf.at[i], dst, sem.at[i + 2]) for i, dst in enumerate((o_out, o_gin))]
-    for cp in loads:
+    ins, outs = refs[:4], refs[4:19]
+    zb, vb, buf, sem = refs[-4:]
+    vals = refs[19:-4]
+    rows = buf.shape[1]
+    load = [pltpu.make_async_copy(ins[i], dst, sem.at[i]) for i, dst in ((2, zb), (3, vb), (0, buf.at[0]), (1, buf.at[1]))]
+    for cp in load:
         cp.start()
+    save = [pltpu.make_async_copy(src, dst, sem.at[4 + i]) for i, (src, dst) in enumerate(zip((buf.at[0], buf.at[1], *vals), outs))]
+    n1g, n1b, qkv, qb, vbias, wo, ob, n2g, n2b, up, ub, down, db = vals
     f = lax.axis_index("fsdp")
-    s, w = zout.shape[2:]
+    s, w = zb.shape[2:]
+    load[0].wait()
     for l in range(2):
         for j in range(4):
-            if j < 3:
-                qkv[l, :, w * j : w * j + w] = zout[3 * l + 2, j].astype(F32)
-            else:
-                wo[l] = zout[3 * l + 2, j].astype(F32)
-            up[l, :, w * j : w * j + w] = zout[3 * l + 1, j].astype(F32)
-            down[l, s * j : s * j + s, :] = zout[3 * l, j].astype(F32)
-    v = pltpu.roll(vout[...], lax.rem(w - s * f, w), 1)
-    u = vout[8:12, :]
-    half = 4 * s * lax.rem(f, 2)
+            up[l, :, w * j : w * j + w] = zb[3 * l + 1, j].astype(F32)
+    save[11].start()
     for l in range(2):
-        for k, ref in enumerate((n1g, n1b, qb, vb, ob, n2g, n2b, db)):
-            ref[l : l + 1, :] = v[12 * l + k : 12 * l + k + 1, :s]
-        row = vout[pl.ds(12 * l + 8 + f // 2, 1), :]
-        ub[l : l + 1, :] = pltpu.roll(jnp.broadcast_to(row, (8, w)), lax.rem(w - half, w), 1)[:1, : 4 * s]
-    for a, b in zip(loads, saves):
-        a.wait()
-        b.start()
-    for b in saves:
-        b.wait()
+        for j in range(4):
+            down[l, s * j : s * j + s, :] = zb[3 * l, j].astype(F32)
+    save[13].start()
+    for l in range(2):
+        for j in range(3):
+            qkv[l, :, w * j : w * j + w] = zb[3 * l + 2, j].astype(F32)
+        wo[l] = zb[3 * l + 2, 3].astype(F32)
+    save[4].start()
+    save[7].start()
+    for i in (0, 1):
+        load[2 + i].wait()
+        save[i].start()
+    load[1].wait()
+    shift = lax.rem(w - 4 * s * lax.rem(f, 2), w)
+    for l in range(2):
+        v = pltpu.roll(vb[l], lax.rem(w - s * f, w), 1)
+        for k, ref in enumerate((n1g, n1b, qb, vbias, ob, n2g, n2b, db)):
+            ref[l : l + 1, :] = v[k : k + 1, :s]
+        row = vb[l, pl.ds(8 + f // 2, 1), :]
+        ub[l : l + 1, :] = pltpu.roll(jnp.broadcast_to(row, (8, w)), shift, 1)[:1, : 4 * s]
+    for i in (2, 3, 5, 6, 8, 9, 10, 12, 14):
+        save[i].start()
+    for cp in save:
+        cp.wait()
 
 
 def finish(out, gin, zout, vout):
     rows, d = out.shape
     s = d // 8
-    t = jax.ShapeDtypeStruct
-    vec = t((2, s), F32)
-    any_, vm = pl.BlockSpec(memory_space=pl.ANY), pl.BlockSpec(memory_space=pltpu.VMEM)
+    shapes = ((2, s), (2, s), (2, s, 3 * d), (2, s), (2, s), (2, s, d), (2, s), (2, s), (2, s), (2, s, 4 * d), (2, 4 * s), (2, 4 * s, d), (2, s))
+    any_ = pl.BlockSpec(memory_space=pl.ANY)
     return pl.pallas_call(
         finish_kernel,
-        out_shape=(
-            t((rows, d), F32), t((rows, d), F32), vec, vec, t((2, s, 3 * d), F32), vec, vec, t((2, s, d), F32), vec, vec, vec,
-            t((2, s, 4 * d), F32), t((2, 4 * s), F32), t((2, 4 * s, d), F32), vec),
-        in_specs=[any_, any_, vm, vm],
-        out_specs=[any_, any_] + [vm] * 13,
-        scratch_shapes=[pltpu.VMEM((2, rows, d), F32), pltpu.SemaphoreType.DMA((4,))],
+        out_shape=[jax.ShapeDtypeStruct(t, F32) for t in ((rows, d), (rows, d), *shapes)],
+        in_specs=[any_] * 4,
+        out_specs=[any_] * 15,
+        scratch_shapes=[pltpu.VMEM(t, F32) for t in shapes]
+        + [pltpu.VMEM(zout.shape, BF16), pltpu.VMEM(vout.shape, F32), pltpu.VMEM((2, rows, d), F32), pltpu.SemaphoreType.DMA((19,))],
     )(out, gin, zout, vout)
 
 

time: 170 us -> 138 us (0.81)
  Pallas kernels: 169 us -> 137 us
    pallas_call x1, Pallas kernels: 163 us -> 133 us  [fused(): pl.pallas_call(functools.partial(fused_kernel, names), out_shape=(s((rows...]
    pallas_call x1, Pallas kernels: 5.55 us -> 3.65 us  [finish(): pl.pallas_call(finish_kernel, out_shape=[jax.ShapeDtypeStruct(t, F32) for...]
where the time goes in v2:
time: 138 us; the launch traced here: 137 us
  Pallas kernels  137 us (99%)
    pallas_call x1, Pallas kernels, fused(): pl.pallas_call(functools.partial(fused_kernel, names), out_shape=(s((rows...  133 us
    pallas_call x1, Pallas kernels, finish(): pl.pallas_call(finish_kernel, out_shape=[jax.ShapeDtypeStruct(t, F32) for...  3.65 us

profile of v2, /device:TPU:0, one launch (start us, length us, event | category | flops | bytes accessed | tf_op | source)
XLA Modules:
  0.0 137.4 jit_solution(6397934949233945625)
XLA Ops:
  0.7 133.0 %shard_map.271 = (f32[1024,384]{1,0:T(8,128)}, f32[1024,384]{1,0:T(8,128)}, bf16[6,4,48,384]{3,2,1,0:T(8,128)(2,1)}, f32[2,12,384]{2,1,0:T(8,128)}) custom-call(f32[1024,384]{1,0:T(8,128)} %refs_0_.1, f32[1024,384]{1,0:T(8,128)} %refs_1_.1, s32[1,1024]{1,0:T(1,128)} %bitcast.1, bf16[2,48]{1,0:T(2,128)(2,1)} %refs_3_.1, bf16[2,48]{1,0:T(2,128)(2,1)} %refs_4_.1, ...), custom_call_target="tpu_custom_call" | custom-call | tf_op jit(solution)/shard_map/pallas_call | solution.py:693
  133.6 3.6 %shard_map.272 = (f32[1024,384]{1,0:T(8,128)}, f32[1024,384]{1,0:T(8,128)}, f32[2,48]{1,0:T(2,128)}, f32[2,48]{1,0:T(2,128)}, f32[2,48,1152]{2,1,0:T(8,128)}, /*...) custom-call(f32[1024,384]{1,0:T(8,128)} %get-tuple-element.19.refs_0, ...), custom_call_target="tpu_custom_call" | custom-call | tf_op jit(solution)/shard_map/pallas_call | solution.py:752

commit v3 on v2

--- a/solution.py
+++ b/solution.py
@@ -9,7 +9,7 @@
 HEADS = 6
 HEAD_DIM = 64
 IMG = 197
-TILE = 256
+TILE, BIG = 256, 512
 norm_eps = 1e-06
 neg_fill = -1e30
 root_half = 0.7071067811865476
@@ -68,7 +68,7 @@
     gain, bias, qb, vb = (vrow(R, l, k) for k in range(4))
 
     def tile(i, c):
-        rows = pl.ds(pl.multiple_of(i * TILE, TILE), TILE)
+        rows = pl.ds(pl.multiple_of(i * BIG, BIG), BIG)
         n, r = norm(src[rows, :])
         R.n1[l, rows, :] = n.astype(BF16)
         R.stats[l, rows, 0:1] = r
@@ -80,7 +80,7 @@
         R.v[l, rows, :] = (proj[:, 768:] + vb).astype(BF16)
         return c
 
-    lax.fori_loop(0, R.rows // TILE, tile, 0)
+    lax.fori_loop(0, R.rows // BIG, tile, 0)
 
 
 def stack_heads(x, low):
@@ -94,10 +94,16 @@
 def twice(x):
     return jnp.concatenate([x, x], 1)
 
-def stage_attend(R, l):
+def when_is(index, hook, name, l, points):
+    for k in points:
+        pl.when(index == k)(functools.partial(hook, name + str(k), l))
+
+
+def stage_attend(R, l, hook):
     low = lowlanes()
 
     def pair(pr, c):
+        when_is(pr, hook, "att", l, (1, 2))
         lanes = pl.ds(pl.multiple_of(pr * 128, 128), 128)
 
         def scores(i, b):
@@ -131,7 +137,7 @@
 
     lax.fori_loop(0, 3, pair, 0)
 
-def stage_mlp(R, l, src, dst):
+def stage_mlp(R, l, src, dst, hook):
     ob, gain, bias, db = (vrow(R, l, k) for k in (4, 5, 6, 7))
     ub = jnp.concatenate([vrow(R, l, 8 + ch) for ch in range(4)], 1)
     last = R.rows // TILE - 1
@@ -151,6 +157,7 @@
         R.midb[...] = mid + db
 
     def tile(i, c):
+        when_is(i, hook, "mlp", l, (1, 2, 3))
         rows = pl.ds(pl.multiple_of(i * TILE, TILE), TILE)
         after = pl.ds(pl.multiple_of(jnp.minimum(i + 1, last) * TILE, TILE), TILE)
         base = R.midb[...]
@@ -167,22 +174,21 @@
     lax.fori_loop(0, last + 1, tile, 0)
 
 
-def stage_mlp_back(R, l):
+def stage_mlp_back(R, l, hook):
     gain = vrow(R, l, 5)
 
     def tile(i, c):
+        when_is(i, hook, "b0t", l, (1, 2, 3))
         rows = pl.ds(pl.multiple_of(i * TILE, TILE), TILE)
         g = R.g[rows, :]
         gl = R.gl[rows, :]
         add_sum(R, l, 7, g)
-        dm = jnp.zeros_like(g)
+        dpre = nt(gl, R.wd[l]) * R.slope[l, rows, :].astype(F32)
         for ch in range(4):
-            cols = slice(384 * ch, 384 * ch + 384)
-            dpre = nt(gl, R.wd[l, cols, :]) * R.slope[l, rows, cols].astype(F32)
-            add_sum(R, l, 8 + ch, dpre)
-            dpre = dpre.astype(BF16)
-            R.slope[l, rows, cols] = dpre
-            dm = dm + nt(dpre, R.wup[l, :, cols])
+            add_sum(R, l, 8 + ch, dpre[:, 384 * ch : 384 * ch + 384])
+        dpre = dpre.astype(BF16)
+        R.slope[l, rows, :] = dpre
+        dm = nt(dpre, R.wup[l])
         n = R.n2[l, rows, :].astype(F32)
         add_sum(R, l, 5, dm * n)
         add_sum(R, l, 6, dm)
@@ -198,13 +204,15 @@
 
 
 def stage_weight_down(R, l):
+    n = R.hidT.shape[1] // 8
+
     def block(b, c):
-        rows = pl.ds(pl.multiple_of(b * n, n), n)
-        R.grad(0, l)[lax.rem(b, 2), b // 2] = nn(R.hidT[l, rows, :], R.gl[...]).astype(BF16)
+        x = nn(R.hidT[l, pl.ds(pl.multiple_of(b * 4 * n, 4 * n), 4 * n), :], R.gl[...]).astype(BF16)
+        for k in range(4):
+            R.grad(0, l)[k % 2, 2 * b + k // 2] = x[n * k : n * k + n]
         return c
 
-    n = R.hidT.shape[1] // 8
-    lax.fori_loop(0, 8, block, 0)
+    lax.fori_loop(0, 2, block, 0)
 
 
 def put_rows(ref, cols, x):
@@ -215,32 +223,37 @@
 
 def stage_weight_up(R, l):
     def block(b, c):
-        cols = pl.ds(pl.multiple_of(b * 256, 256), 256)
+        cols = pl.ds(pl.multiple_of(b * 512, 512), 512)
         put_rows(R.grad(1, l), cols, nn(R.mT[l], R.slope[l, :, cols]))
         return c
 
-    lax.fori_loop(0, 6, block, 0)
+    lax.fori_loop(0, 3, block, 0)
+
+
+def put_block(R, l, j, x):
+    n = x.shape[0] // 8
+    ref = R.grad(2, l)
+    for b in range(8):
+        ref[j, b % 2, b // 2] = x[n * b : n * b + n].astype(BF16)
 
 
 def stage_weight_out(R, l):
-    put_rows(R.grad(2, l), slice(1152, 1536), nn(R.attT[l], R.gml[...]))
-
-
-def stage_weight_qkv(R, l):
-    def block(b, c):
-        cols = pl.ds(pl.multiple_of(b * 384, 128), 384)
-        put_rows(R.grad(2, l), cols, nn(R.aT[l], R.dproj[:, cols]))
-        return c
-
-    lax.fori_loop(0, 3, block, 0)
-
-
-def stage_attend_back(R, l):
+    put_block(R, l, 3, nn(R.attT[l], R.gml[...]))
+
+
+def weight_qkv(R, l, pr):
+    off = pr * 128 if isinstance(pr, int) else pl.multiple_of(pr * 128, 128)
+    put_block(R, l, pr, nn(R.aT[l], jnp.concatenate([R.dproj[:, pl.ds(384 * k + off, 128)] for k in range(3)], 1)))
+
+
+def stage_attend_back(R, l, hook, pairs=None):
     low = lowlanes()
 
     def pair(pr, c):
-        off = pl.multiple_of(pr * 128, 128)
+        off = pr * 128 if isinstance(pr, int) else pl.multiple_of(pr * 128, 128)
         lanes = pl.ds(off, 128)
+        if pairs is None:
+            when_is(pr, hook, "pr", l, (1, 2))
         R.dk[...] = jnp.zeros((R.rows, 128), F32)
         R.dv[...] = jnp.zeros((R.rows, 128), F32)
 
@@ -279,15 +292,19 @@
         R.vacc[12 * l + 3, :, lanes] += fold8(dv)
         R.dproj[:, pl.ds(384 + off, 128)] = (R.dk[...] * (1.0 / LOG2E)).astype(BF16)
         R.dproj[:, pl.ds(768 + off, 128)] = dv.astype(BF16)
+        weight_qkv(R, l, pr)
         return c
 
-    lax.fori_loop(0, 3, pair, 0)
-
-def stage_qkv_back(R, l):
+    if pairs is None:
+        lax.fori_loop(0, 3, pair, 0)
+    else:
+        pair(pairs, 0)
+
+def stage_qkv_back(R, l, lo=0, hi=2):
     gain = vrow(R, l, 0)
 
     def tile(i, c):
-        rows = pl.ds(pl.multiple_of(i * TILE, TILE), TILE)
+        rows = pl.ds(pl.multiple_of(i * BIG, BIG), BIG)
         da = nt(R.dproj[rows, :], R.wqkv[l])
         n = R.n1[l, rows, :].astype(F32)
         add_sum(R, l, 0, da * n)
@@ -298,7 +315,7 @@
             R.gl[rows, :] = g.astype(BF16)
         return c
 
-    lax.fori_loop(0, R.rows // TILE, tile, 0)
+    lax.fori_loop(lo, hi, tile, 0)
 
 
 def stage_segments(R):
@@ -328,25 +345,30 @@
         hook("qkv", l)
         stage_qkv(R, l, streams[l])
         hook("att", l)
-        stage_attend(R, l)
+        stage_attend(R, l, hook)
         hook("mlp", l)
-        stage_mlp(R, l, streams[l], streams[l + 1])
+        stage_mlp(R, l, streams[l], streams[l + 1], hook)
     hook("fwd", 0)
     stage_cotangent(R)
     for l in (1, 0):
         stage_weight_down(R, l)
         hook("dD", l)
-        stage_mlp_back(R, l)
+        stage_mlp_back(R, l, hook)
         hook("b0", l)
         stage_weight_up(R, l)
         hook("dU", l)
         stage_weight_out(R, l)
         hook("dO", l)
-        stage_attend_back(R, l)
-        hook("batt", l)
-        stage_weight_qkv(R, l)
-        hook("dA", l)
-        stage_qkv_back(R, l)
+        if l:
+            stage_attend_back(R, l, hook)
+            hook("pair2", l)
+        else:
+            for pr in range(3):
+                stage_attend_back(R, l, hook, pr)
+                hook("pair" + str(pr), l)
+        stage_qkv_back(R, l, 0, 1)
+        hook("half", l)
+        stage_qkv_back(R, l, 1, 2)
         hook("b1", l)
 
 
@@ -374,15 +396,19 @@
     s, t = d // 8, f // 8
     return dict(
         wqkv=v((2, d, 3 * d), BF16), wo=v((2, d, d), BF16), wup=v((2, d, f), BF16), wd=v((2, f, d), BF16),
-        pk=v((24, 128), F32), mine=v((24, d), F32), gat=v((8, 24, d), F32), vec=v((24, d), F32),
-        dD=v((2, 4, t, d), BF16), dU=v((2, 4, s, f), BF16), dA=v((2, 4, s, f), BF16),
-        pD=v((2, 4, t, d), BF16), pU=v((2, 4, s, f), BF16), pA=v((2, 4, s, f), BF16),
-        xD=v((2, 3, t, d), BF16), xU=v((2, 3, s, f), BF16), xA=v((2, 3, s, f), BF16),
-        zb=v((6, 4, s, d), BF16), zr=v((6, 4, s, d), BF16), zs=v((6, s, d), BF16),
-        v0=v((2, 12, d), F32), v1=v((2, 12, d), F32), v2=v((2, 12, d), F32), v3=v((2, 3, 12, d), F32), v4=v((2, 4, 12, d), F32), vs=v((2, 12, d), F32), vl=dma((2,)),
-        loc=dma((9,)), ags=dma((9, 7)), agr=dma((9, 7)), s1s=dma((8,)), s1r=dma((8,)), s2s=dma((8, 3)), s2r=dma((8, 3)),
-        s3s=dma((8, 3)), s3r=dma((8, 3)), s4s=dma((6, 3)), s4r=dma((6, 3)), s4l=dma((6,)),
+        pk=v((24, 128), F32), mine=v((24, d), BF16), gat=v((8, 24, d), BF16), vec=v((24, d), F32),
+        dD=v((2, 4, t, d), BF16), dU=v((2, 4, s, f), BF16), dA=v((4, 2, 4, s, d), BF16),
+        pD=v((2, 4, t, d), BF16), pU=v((2, 4, s, f), BF16), pA=v((8, 4, s, d), BF16),
+        xD=v((2, 3, t, d), BF16), xU=v((2, 3, s, f), BF16), xA=v((8, 3, s, d), BF16),
+        zb=v((4, 4, s, d), BF16), zr=v((4, 3, s, d), BF16), zs=v((4, s, d), BF16),
+        yb=v((8, s, d), BF16), yr=v((8, 3, s, d), BF16), ys=v((8, s, d), BF16),
+        v0=v((2, 12, d), F32), v1=v((2, 12, d), F32), v2=v((2, 12, d), F32), v3=v((2, 3, 12, d), F32), v4=v((2, 4, 12, d), F32),
+        vs=v((2, 12, d), F32), vl=dma((2,)), loc=dma((9,)), ags=dma((9,)), agr=dma((9, 3)),
+        s1s=dma((14,)), s1r=dma((14,)), s2s=dma((14,)), s2r=dma((14,)), s3s=dma((14,)), s3r=dma((14,)), s4s=dma((12,)), s4r=dma((12,)),
     )
+
+
+OWNER = (0, 3, 1, 2)
 
 
 class Comm:
@@ -397,7 +423,10 @@
         dy = 2 - 4 * (self.p // 2)
         self.chip = (self.p, self.p + dx, self.p + dy, self.p + dx + dy)
         self.core = 1 - self.c
-        self.open, self.first = [], {}
+        self.partner = self.dev(self.p, self.core)
+        self.steps = (
+            self.own, self.relay, self.diagonal, self.have, self.step1, self.step2, self.step3, self.step4, self.step5,
+            self.vec1, self.vec2, self.vec3, self.vec4)
 
     def dev(self, chip, core):
         return {"fsdp": 2 * chip + core}
@@ -405,15 +434,14 @@
     def rep(self, d):
         return lax.rem(self.z + d, 4)
 
-    def push(self, src, dst, ss, rs, dev, keep=True):
-        cp = pltpu.make_async_remote_copy(src, dst, ss, rs, device_id=dev, device_id_type=MESH)
-        cp.start()
-        if keep:
-            self.open.append(cp)
-        return cp
-
-    def arrive(self, dst, ss, rs, dev):
-        pltpu.make_async_remote_copy(dst, dst, ss, rs, device_id=dev, device_id_type=MESH).wait_recv()
+    def push(self, src, dst, ss, rs, dev):
+        pltpu.make_async_remote_copy(src, dst, ss, rs, device_id=dev, device_id_type=MESH).start()
+
+    def got(self, ref, sem):
+        pltpu.make_async_remote_copy(ref, ref, sem, sem, device_id=self.partner, device_id_type=MESH).wait_recv()
+
+    def sent(self, ref, sem):
+        pltpu.make_async_remote_copy(ref, ref, sem, sem, device_id=self.partner, device_id_type=MESH).wait_send()
 
     def barrier(self):
         bar = pltpu.get_barrier_semaphore()
@@ -422,19 +450,27 @@
         pl.semaphore_wait(bar, 7)
 
     def peers(self):
-        out = [self.dev(self.p, self.core)]
+        out = [self.partner]
         out += [self.dev(self.chip[k], self.c) for k in (1, 2, 3)]
         out += [{"rep": self.rep(d)} for d in (1, 2, 3)]
         return out
 
-    def slot(self, i, f):
+    def shards(self, i, f, n=1):
         R = self.R
         if i == 0:
-            return R.gat.at[f]
+            return R.gat.at[pl.ds(f, n)]
         l, k = (i - 1) // 4, (i - 1) % 4
         ref = (R.wqkv, R.wo, R.wup, R.wd)[k]
-        n = ref.shape[1] // 8
-        return ref.at[l, pl.ds(pl.multiple_of(f * n, n), n)]
+        m = ref.shape[1] // 8
+        return ref.at[l, pl.ds(pl.multiple_of(f * m, m), n * m)]
+
+    def half(self, i, f, h):
+        R = self.R
+        l, k = (i - 1) // 4, (i - 1) % 4
+        ref = (R.wqkv, R.wo, R.wup, R.wd)[k]
+        m, w = ref.shape[1] // 8, ref.shape[2]
+        cut = w // 256 * 128
+        return ref.at[l, pl.ds(pl.multiple_of(f * m, m), m), pl.ds(0, cut) if h == 0 else pl.ds(cut, w - cut)]
 
     def source(self, i):
         R = self.R
@@ -443,126 +479,187 @@
         l, k = (i - 1) // 4, (i - 1) % 4
         return (R.sqkv, R.so, R.sup, R.sd)[k].at[l]
 
-    def gather_start(self, i):
-        R, src, dst = self.R, self.source(i), self.slot(i, self.f)
-        self.push(src, dst, R.ags.at[i, 1], R.agr.at[i, 1], self.dev(self.chip[1], self.c))
-        self.push(src, dst, R.ags.at[i, 2], R.agr.at[i, 2], self.dev(self.chip[2], self.c))
-        self.push(src, dst, R.ags.at[i, 3], R.agr.at[i, 3], self.dev(self.chip[3], self.c))
-        self.push(src, dst, R.ags.at[i, 0], R.agr.at[i, 0], self.dev(self.p, self.core))
+    def target(self, i):
+        return self.R.gat.at[self.f] if i == 0 else self.shards(i, self.f)
+
+    def own(self, i):
+        R, src, dst = self.R, self.source(i), self.target(i)
+        for k in (1, 2, 3) if i < 2 else (1, 2):
+            self.push(src, dst, R.ags.at[i], R.agr.at[i, 0], self.dev(self.chip[k], self.c))
+        self.push(src, dst, R.ags.at[i], R.agr.at[i, 2], self.partner)
         pltpu.make_async_copy(src, dst, R.loc.at[i]).start()
 
-    def gather_forward(self, i):
-        R = self.R
-        for k in (1, 2, 3):
-            own = self.slot(i, 2 * self.chip[k] + self.c)
-            self.arrive(own, R.ags.at[i, k], R.agr.at[i, k], self.dev(self.chip[k], self.c))
-            self.push(own, own, R.ags.at[i, 3 + k], R.agr.at[i, 3 + k], self.dev(self.p, self.core))
-
-    def gather_finish(self, i):
-        R = self.R
-        pltpu.make_async_copy(self.source(i), self.slot(i, self.f), R.loc.at[i]).wait()
-        for k in (0, 1, 2, 3):
-            j = 0 if k == 0 else 3 + k
-            dst = self.slot(i, 2 * self.chip[k] + self.core)
-            self.arrive(dst, R.ags.at[i, j], R.agr.at[i, j], self.dev(self.p, self.core))
+    def forward(self, i, k):
+        here = self.shards(i, 2 * self.chip[k] + self.c)
+        self.push(here, here, self.R.ags.at[i], self.R.agr.at[i, 2], self.partner)
+
+    def relay(self, i):
+        R = self.R
+        self.got(self.shards(i, 0, 3 if i < 2 else 2), R.agr.at[i, 0])
+        if i >= 2:
+            for h, (src, to) in enumerate(((1, 2), (2, 1))):
+                here = self.half(i, 2 * self.chip[src] + self.c, h)
+                self.push(here, here, R.ags.at[i], R.agr.at[i, 1], self.dev(self.chip[to], self.c))
+        for k in (1, 2, 3) if i < 2 else (1, 2):
+            self.forward(i, k)
+
+    def diagonal(self, i):
+        self.got(self.shards(i, 0), self.R.agr.at[i, 1])
+        self.forward(i, 3)
+
+    def have(self, i):
+        R = self.R
+        pltpu.make_async_copy(self.source(i), self.target(i), R.loc.at[i]).wait()
+        self.got(self.shards(i, 0, 4), R.agr.at[i, 2])
 
     def grads(self, t):
-        R, l = self.R, t // 3
-        d, p, x = ((R.dD, R.pD, R.xD), (R.dU, R.pU, R.xU), (R.dA, R.pA, R.xA))[t % 3]
-        return d, p.at[l], x.at[l]
+        R = self.R
+        if t < 4:
+            l = t // 2
+            d, p, x = ((R.dD, R.pD, R.xD), (R.dU, R.pU, R.xU))[t % 2]
+            return d, p.at[l], x.at[l]
+        return R.dA.at[t % 4], R.pA.at[t - 4], R.xA.at[t - 4]
 
     def step1(self, t):
         R = self.R
         d, p, x = self.grads(t)
-        self.first[t] = self.push(d.at[self.core], p, R.s1s.at[t], R.s1r.at[t], self.dev(self.p, self.core), False)
+        self.push(d.at[self.core], p, R.s1s.at[t], R.s1r.at[t], self.partner)
 
     def step2(self, t):
         R = self.R
         d, p, x = self.grads(t)
-        self.first[t].wait()
+        self.sent(d.at[self.core], R.s1s.at[t])
+        self.got(p, R.s1r.at[t])
         for k in (3, 1, 2, 0):
             ch = self.chip[k]
             p[ch] = (d[self.c, ch].astype(F32) + p[ch].astype(F32)).astype(BF16)
             if k:
-                self.push(p.at[ch], x.at[k - 1], R.s2s.at[t, k - 1], R.s2r.at[t, k - 1], self.dev(ch, self.c))
+                self.push(p.at[ch], x.at[k - 1], R.s2s.at[t], R.s2r.at[t], self.dev(ch, self.c))
 
     def step3(self, t):
         R = self.R
         d, p, x = self.grads(t)
-        for k in (1, 2, 3):
-            self.arrive(x.at[k - 1], R.s2s.at[t, k - 1], R.s2r.at[t, k - 1], self.dev(self.chip[k], self.c))
-        s = R.zb.shape[2]
-        w = R.zb.shape[3]
-        for j in range(4):
-            at = (slice(s * j, s * j + s), slice(None)) if t % 3 == 0 else (slice(None), slice(w * j, w * j + w))
+        self.got(x, R.s2r.at[t])
+        self.sent(x, R.s2s.at[t])
+
+        def total(*at):
             tot = p[(self.p, *at)].astype(F32)
             for k in range(3):
                 tot = tot + x[(k, *at)].astype(F32)
-            R.zb[t, j] = tot.astype(BF16)
+            return tot.astype(BF16)
+
+        s, w = R.zb.shape[2:]
+        if t >= 4:
+            u, owner = t - 4, OWNER[t % 4]
+            R.yb[u] = total(slice(None), slice(None))
+
+            @pl.when(self.z != owner)
+            def _():
+                slot = lax.rem(self.z + 3 - owner, 4)
+                self.push(R.yb.at[u], R.yr.at[u, slot], R.s3s.at[t], R.s3r.at[t], {"rep": owner})
+
+            return
+        for j in range(4):
+            rows, cols = slice(s * j, s * j + s), slice(w * j, w * j + w)
+            R.zb[t, j] = total(rows, slice(None)) if t % 2 == 0 else total(slice(None), cols)
         for e in (1, 2, 3):
             r = self.rep(e)
-            self.push(R.zb.at[t, r], R.zr.at[t, self.z], R.s3s.at[t, e - 1], R.s3r.at[t, e - 1], {"rep": r})
+            self.push(R.zb.at[t, r], R.zr.at[t, e - 1], R.s3s.at[t], R.s3r.at[t], {"rep": r})
+
+    def place(self, t):
+        return (t % 2 + 3 * (t // 2), None) if t < 4 else (3 * ((t - 4) // 4) + 2, t % 4)
 
     def step4(self, t):
         R = self.R
+        row, j = self.place(t)
+        if t >= 4:
+            u, owner = t - 4, OWNER[t % 4]
+
+            @pl.when(self.z == owner)
+            def _():
+                self.got(R.yr.at[u], R.s3r.at[t])
+                tot = R.yb[u].astype(F32)
+                for k in range(3):
+                    tot = tot + R.yr[u, k].astype(F32)
+                R.ys[u] = tot.astype(BF16)
+                here = R.zout.at[row, j]
+                for e in (1, 2, 3):
+                    self.push(R.ys.at[u], here, R.s4s.at[t], R.s4r.at[t], {"rep": (owner + e) % 4})
+                pltpu.make_async_copy(R.ys.at[u], here, R.s4r.at[t]).start()
+
+            return
+        self.got(R.zr.at[t], R.s3r.at[t])
+        self.sent(R.zr.at[t], R.s3s.at[t])
         tot = R.zb[t, self.z].astype(F32)
+        for k in range(3):
+            tot = tot + R.zr[t, k].astype(F32)
+        R.zs[t] = tot.astype(BF16)
+        here = R.zout.at[row, self.z]
         for e in (1, 2, 3):
-            r = self.rep(4 - e)
-            self.arrive(R.zr.at[t, r], R.s3s.at[t, e - 1], R.s3r.at[t, e - 1], {"rep": r})
-            tot = tot + R.zr[t, r].astype(F32)
-        R.zs[t] = tot.astype(BF16)
-        here = R.zout.at[t, self.z]
+            self.push(R.zs.at[t], here, R.s4s.at[t], R.s4r.at[t], {"rep": self.rep(e)})
+        pltpu.make_async_copy(R.zs.at[t], here, R.s4r.at[t]).start()
+
+    def step5(self, t):
+        R = self.R
+        row, j = self.place(t)
+        if t >= 4:
+            u, owner = t - 4, OWNER[t % 4]
+            self.got(R.zout.at[row, j], R.s4r.at[t])
+
+            @pl.when(self.z == owner)
+            def _():
+                self.sent(R.yr.at[u], R.s4s.at[t])
+
+            @pl.when(self.z != owner)
+            def _():
+                self.sent(R.yb.at[u], R.s3s.at[t])
+
+            return
+        self.got(R.zout.at[row], R.s4r.at[t])
+        self.sent(R.zr.at[t], R.s4s.at[t])
+
+    def vec1(self, l):
+        R, t = self.R, 12 + l
+        R.v0[l] = jnp.sum(R.vacc[12 * l : 12 * l + 12], axis=1)
+        self.push(R.v0.at[l], R.v1.at[l], R.s1s.at[t], R.s1r.at[t], self.partner)
+
+    def vec2(self, l):
+        R, t = self.R, 12 + l
+        self.got(R.v1.at[l], R.s1r.at[t])
+        self.sent(R.v0.at[l], R.s1s.at[t])
+        R.v2[l] = R.v0[l] + R.v1[l]
+        for k in (1, 2, 3):
+            self.push(R.v2.at[l], R.v3.at[l, k - 1], R.s2s.at[t], R.s2r.at[t], self.dev(self.chip[k], self.c))
+
+    def vec3(self, l):
+        R, t = self.R, 12 + l
+        self.got(R.v3.at[l], R.s2r.at[t])
+        self.sent(R.v3.at[l], R.s2s.at[t])
+        tot = R.v2[l]
+        for k in (1, 2, 3):
+            tot = tot + R.v3[l, k - 1]
+        R.v4[l, self.z] = tot
+        here = R.v4.at[l, self.z]
         for e in (1, 2, 3):
-            self.push(R.zs.at[t], here, R.s4s.at[t, e - 1], R.s4r.at[t, e - 1], {"rep": self.rep(e)})
-        pltpu.make_async_copy(R.zs.at[t], here, R.s4l.at[t]).start()
-
-    def step5(self, t):
-        R = self.R
-        for e in (1, 2, 3):
-            r = self.rep(4 - e)
-            self.arrive(R.zout.at[t, r], R.s4s.at[t, e - 1], R.s4r.at[t, e - 1], {"rep": r})
-        pltpu.make_async_copy(R.zs.at[t], R.zout.at[t, self.z], R.s4l.at[t]).wait()
+            self.push(here, here, R.s3s.at[t], R.s3r.at[t], {"rep": self.rep(e)})
+
+    def vec4(self, l):
+        R, t = self.R, 12 + l
+        self.got(R.v3.at[l], R.s3r.at[t])
+        self.sent(R.v3.at[l], R.s3s.at[t])
+        R.vs[l] = (R.v4[l, 0] + R.v4[l, 1]) + (R.v4[l, 2] + R.v4[l, 3])
+        pltpu.make_async_copy(R.vs.at[l], R.vout.at[l], R.vl.at[l]).start()
 
     def late_sends(self):
-        for cp in self.open:
-            cp.wait_send()
+        for i in range(9):
+            self.sent(self.shards(i, 0, 7), self.R.ags.at[i])
 
     def late_io(self, save):
-        pltpu.make_async_copy(self.R.xb, self.R.out, self.R.io.at[1]).wait()
+        R = self.R
+        pltpu.make_async_copy(R.xb, R.out, R.io.at[1]).wait()
         save.wait()
         for l in range(2):
-            pltpu.make_async_copy(self.R.vs.at[l], self.R.vout.at[l], self.R.vl.at[l]).wait()
-
-    def vec1(self, l):
-        R = self.R
-        R.v0[l] = jnp.sum(R.vacc[12 * l : 12 * l + 12], axis=1)
-        self.push(R.v0.at[l], R.v1.at[l], R.s1s.at[6 + l], R.s1r.at[6 + l], self.dev(self.p, self.core))
-
-    def vec2(self, l):
-        R, t = self.R, 6 + l
-        self.arrive(R.v1.at[l], R.s1s.at[t], R.s1r.at[t], self.dev(self.p, self.core))
-        R.v2[l] = R.v0[l] + R.v1[l]
-        for k in (1, 2, 3):
-            self.push(R.v2.at[l], R.v3.at[l, k - 1], R.s2s.at[t, k - 1], R.s2r.at[t, k - 1], self.dev(self.chip[k], self.c))
-
-    def vec3(self, l):
-        R, t = self.R, 6 + l
-        tot = R.v2[l]
-        for k in (1, 2, 3):
-            self.arrive(R.v3.at[l, k - 1], R.s2s.at[t, k - 1], R.s2r.at[t, k - 1], self.dev(self.chip[k], self.c))
-            tot = tot + R.v3[l, k - 1]
-        R.v4[l, self.z] = tot
-        for e in (1, 2, 3):
-            here = R.v4.at[l, self.z]
-            self.push(here, here, R.s3s.at[t, e - 1], R.s3r.at[t, e - 1], {"rep": self.rep(e)})
-
-    def vec4(self, l):
-        R, t = self.R, 6 + l
-        for e in (1, 2, 3):
-            r = self.rep(4 - e)
-            self.arrive(R.v4.at[l, r], R.s3s.at[t, e - 1], R.s3r.at[t, e - 1], {"rep": r})
-        R.vs[l] = (R.v4[l, 0] + R.v4[l, 1]) + (R.v4[l, 2] + R.v4[l, 3])
-        pltpu.make_async_copy(R.vs.at[l], R.vout.at[l], R.vl.at[l]).start()
+            pltpu.make_async_copy(R.vs.at[l], R.vout.at[l], R.vl.at[l]).wait()
 
     def place_vectors(self):
         R = self.R
@@ -574,7 +671,7 @@
         row = lax.broadcasted_iota(jnp.int32, (128, 384), 0)
         col = lax.broadcasted_iota(jnp.int32, (128, 384), 1)
         put = (col == row + n * self.f) & (row < n)
-        R.mine[...] = nn(R.pk[...].astype(BF16), put.astype(F32).astype(BF16))
+        R.mine[...] = nn(R.pk[...].astype(BF16), put.astype(F32).astype(BF16)).astype(BF16)
         ub = R.small[8]
         w = ub.shape[1]
         row = lax.broadcasted_iota(jnp.int32, (w, 384), 0)
@@ -583,7 +680,7 @@
         moved = nn(ub[...], put)
         for l in range(2):
             for h in range(4):
-                R.mine[12 * l + 8 + h : 12 * l + 9 + h, :] = moved[l : l + 1, :] * (self.p == h).astype(F32)
+                R.mine[12 * l + 8 + h : 12 * l + 9 + h, :] = (moved[l : l + 1, :] * (self.p == h).astype(F32)).astype(BF16)
 
 
 def single_kernel(names, *refs):
@@ -604,7 +701,7 @@
     return pl.pallas_call(
         functools.partial(single_kernel, names),
         out_shape=(
-            s((rows, d), F32), s((rows, d), F32), s((2, 2, 4, d // 8, f), BF16), s((2, 2, 4, d // 8, f), BF16),
+            s((rows, d), F32), s((rows, d), F32), s((2, 4, 2, 4, d // 8, d), BF16), s((2, 2, 4, d // 8, f), BF16),
             s((2, 2, 4, f // 8, d), BF16), s((24, d), F32)),
         in_specs=[pl.BlockSpec(memory_space=pltpu.VMEM)] * 8,
         out_specs=[pl.BlockSpec(memory_space=pltpu.VMEM)] * 6,
@@ -613,21 +710,44 @@
     )(x, cot, seg, vec, wqkv, wo, wup, wd)
 
 
+OWN, RELAY, DIAG, HAVE, S1, S2, S3, S4, S5, V1, V2, V3, V4 = range(13)
 PLAN = {
-    ("dD", 1): (("step1", 3),),
-    ("b0", 1): (("step2", 3),),
-    ("dU", 1): (("step1", 4),),
-    ("batt", 1): (("step2", 4), ("step3", 3)),
-    ("dA", 1): (("step1", 5),),
-    ("b1", 1): (("vec1", 1), ("step2", 5), ("step4", 3)),
-    ("dD", 0): (("step1", 0), ("step3", 4), ("vec2", 1)),
-    ("b0", 0): (("step2", 0), ("step3", 5), ("step4", 4), ("vec3", 1)),
-    ("dU", 0): (("step1", 1),),
-    ("dO", 0): (("step2", 1),),
-    ("batt", 0): (("step3", 0), ("step4", 5), ("vec4", 1)),
-    ("dA", 0): (("step1", 2),),
-    ("b1", 0): (("vec1", 0), ("step2", 2), ("step3", 1), ("step4", 0)),
-    ("tail", 0): (("vec2", 0), ("step3", 2), ("vec3", 0), ("step4", 1), ("step4", 2), ("vec4", 0)),
+    ("start", 0): ((OWN, 0), (OWN, 1), (OWN, 2), (OWN, 3), (OWN, 4),),
+    ("qkv", 0): ((RELAY, 0), (RELAY, 1), (HAVE, 0), (HAVE, 1),),
+    ("att", 0): ((RELAY, 2), (RELAY, 3),),
+    ("att1", 0): ((RELAY, 4), (OWN, 5),),
+    ("att2", 0): ((DIAG, 2), (DIAG, 3), (OWN, 6),),
+    ("mlp", 0): ((DIAG, 4), (HAVE, 2), (HAVE, 3), (HAVE, 4),),
+    ("mlp1", 0): ((RELAY, 5), (OWN, 7),),
+    ("mlp2", 0): ((RELAY, 6),),
+    ("mlp3", 0): ((DIAG, 5), (OWN, 8),),
+    ("qkv", 1): ((HAVE, 5),),
+    ("att", 1): ((RELAY, 7), (DIAG, 6),),
+    ("att1", 1): ((RELAY, 8),),
+    ("att2", 1): ((DIAG, 7),),
+    ("mlp", 1): ((DIAG, 8), (HAVE, 6), (HAVE, 7), (HAVE, 8),),
+    ("dD", 1): ((S1, 2),),
+    ("b0t1", 1): ((S2, 2),),
+    ("dU", 1): ((S1, 3),),
+    ("dO", 1): ((S1, 11),),
+    ("pr1", 1): ((S3, 2), (S2, 3), (S2, 11), (S1, 8),),
+    ("pr2", 1): ((S2, 8), (S1, 9),),
+    ("pair2", 1): ((S4, 2), (S2, 9), (S1, 10),),
+    ("half", 1): ((S2, 10),),
+    ("b1", 1): ((V1, 1),),
+    ("dD", 0): ((S1, 0), (V2, 1), (S3, 3),),
+    ("b0t1", 0): ((S3, 11),),
+    ("b0t2", 0): ((S2, 0), (S3, 8),),
+    ("b0t3", 0): ((S4, 3), (S3, 9),),
+    ("b0", 0): ((S3, 10), (V3, 1), (S4, 11),),
+    ("dU", 0): ((S1, 1), (S4, 8),),
+    ("dO", 0): ((S1, 7), (S4, 9), (S2, 1), (S3, 0),),
+    ("pair0", 0): ((S2, 7), (S1, 4), (S4, 10), (V4, 1),),
+    ("pair1", 0): ((S2, 4), (S1, 5),),
+    ("pair2", 0): ((S3, 1), (S2, 5), (S1, 6), (S4, 0),),
+    ("half", 0): ((S3, 7), (S2, 6),),
+    ("b1", 0): ((V1, 0), (S3, 4),),
+    ("tail", 0): ((V2, 0), (S3, 5), (S3, 6), (V3, 0), (S4, 1), (S4, 7), (S4, 4), (S4, 5), (S4, 6), (V4, 0), (S5, 2), (S5, 3), (S5, 8), (S5, 9), (S5, 10), (S5, 11), (S5, 0), (S5, 7), (S5, 1), (S5, 4), (S5, 5), (S5, 6),),
 }
 
 
@@ -645,40 +765,22 @@
     C = Comm(R)
     C.place_vectors()
     C.barrier()
-    for i in range(9):
-        C.gather_start(i)
-    load.wait()
 
     def hook(name, l):
-        t = 3 * l
-        if name == "qkv":
-            if l == 0:
-                C.gather_forward(0)
-            C.gather_forward(1 + 4 * l)
-            if l == 0:
-                C.gather_finish(0)
-                R.vec[...] = jnp.sum(R.gat[...], axis=0)
-            C.gather_finish(1 + 4 * l)
-        if name == "att":
-            C.gather_forward(2 + 4 * l)
-        if name == "mlp":
-            C.gather_forward(3 + 4 * l)
-            C.gather_forward(4 + 4 * l)
-            for k in (2, 3, 4):
-                C.gather_finish(k + 4 * l)
+        for item in PLAN.get((name, l), ()):
+            C.steps[item[0]](item[1])
+        if (name, l) == ("qkv", 0):
+            R.vec[...] = jnp.sum(R.gat[...].astype(F32), axis=0)
         if name == "fwd":
             pltpu.make_async_copy(R.xb, R.out, R.io.at[1]).start()
             cot.wait()
-        for what, k in PLAN.get((name, l), ()):
-            getattr(C, what)(k)
-
+
+    hook("start", 0)
+    load.wait()
     compute(R, (R.xb, R.mid, R.xb), hook)
     save = pltpu.make_async_copy(R.g, R.gin, R.io.at[2])
     save.start()
-    for what, k in PLAN["tail", 0]:
-        getattr(C, what)(k)
-    for t in (3, 4, 5, 0, 1, 2):
-        C.step5(t)
+    hook("tail", 0)
     C.late_sends()
     C.late_io(save)
 
@@ -723,7 +825,8 @@
     save[13].start()
     for l in range(2):
         for j in range(3):
-            qkv[l, :, w * j : w * j + w] = zb[3 * l + 2, j].astype(F32)
+            for k in range(3):
+                qkv[l, :, w * k + 128 * j : w * k + 128 * j + 128] = zb[3 * l + 2, j, :, 128 * k : 128 * k + 128].astype(F32)
         wo[l] = zb[3 * l + 2, 3].astype(F32)
     save[4].start()
     save[7].start()
@@ -775,12 +878,14 @@
     vecs = jnp.stack([gather(a) for a in (n1g, n1b, qb, vb, ob, n2g, n2b, db)], 1)
     vec = jnp.concatenate([vecs, gather(ub).reshape(2, 4, d)], 1).astype(F32).reshape(24, d)
     out, gin, da, du, dd, vg = single(x, cot, seg[None], vec, gather(qkv), gather(wo), gather(up), gather(down))
-    da, du, dd = (jnp.swapaxes(a, 1, 2).reshape(2, -1, a.shape[-1]).astype(F32) for a in (da, du, dd))
-    da, du, dd = scatter(da), scatter(du), scatter(dd)
+    du, dd = (jnp.swapaxes(a, 1, 2).reshape(2, -1, a.shape[-1]).astype(F32) for a in (du, dd))
+    da = jnp.transpose(da, (0, 3, 2, 4, 1, 5)).reshape(2, d, 4, d).astype(F32)
+    dqkv = jnp.swapaxes(da[:, :, :3].reshape(2, d, 3, 3, d // 3), 2, 3).reshape(2, d, 3 * d)
+    dqkv, dwo, du, dd = scatter(dqkv), scatter(da[:, :, 3]), scatter(du), scatter(dd)
     vg = vg.reshape(2, 12, d)
     g = [scatter(vg[:, k]) for k in range(8)]
     gub = scatter(vg[:, 8:].reshape(2, 4 * d))
-    return (out, gin, g[0], g[1], da[..., : 3 * d], g[2], g[3], da[..., 3 * d :], g[4], g[5], g[6], du, gub, dd, g[7])
+    return (out, gin, g[0], g[1], dqkv, g[2], g[3], dwo, g[4], g[5], g[6], du, gub, dd, g[7])
 
 
 def solution(mesh):

time: 138 us -> 122 us (0.88)
  Pallas kernels: 137 us -> 121 us
    pallas_call x1, Pallas kernels: 133 us -> 118 us  [fused(): pl.pallas_call(functools.partial(fused_kernel, names), out_shape=(s((rows...]
where the time goes in v3:
time: 122 us
  Pallas kernels  121 us (99%)
    pallas_call x1, Pallas kernels, fused(): pl.pallas_call(functools.partial(fused_kernel, names), out_shape=(s((rows...  118 us
    pallas_call x1, Pallas kernels, finish(): pl.pallas_call(finish_kernel, out_shape=[jax.ShapeDtypeStruct(t, F32) for...  3.65 us

profile of v3, /device:TPU:0, one launch (start us, length us, event | category | flops | bytes accessed | tf_op | source)
XLA Modules:
  0.0 122.1 jit_solution(7826816692706745846)
XLA Ops:
  0.7 117.6 %shard_map.271 = (f32[1024,384]{1,0:T(8,128)}, f32[1024,384]{1,0:T(8,128)}, bf16[6,4,48,384]{3,2,1,0:T(8,128)(2,1)}, f32[2,12,384]{2,1,0:T(8,128)}) custom-call(f32[1024,384]{1,0:T(8,128)} %refs_0_.1, f32[1024,384]{1,0:T(8,128)} %refs_1_.1, s32[1,1024]{1,0:T(1,128)} %bitcast.1, bf16[2,48]{1,0:T(2,128)(2,1)} %refs_3_.1, bf16[2,48]{1,0:T(2,128)(2,1)} %refs_4_.1, ...), custom_call_target="tpu_custom_call" | custom-call | tf_op jit(solution)/shard_map/pallas_call | solution.py:795
  118.2 3.6 %shard_map.272 = (f32[1024,384]{1,0:T(8,128)}, f32[1024,384]{1,0:T(8,128)}, f32[2,48]{1,0:T(2,128)}, f32[2,48]{1,0:T(2,128)}, f32[2,48,1152]{2,1,0:T(8,128)}, /*...) custom-call(f32[1024,384]{1,0:T(8,128)} %get-tuple-element.19.refs_0, ...), custom_call_target="tpu_custom_call" | custom-call | tf_op jit(solution)/shard_map/pallas_call | solution.py:855

commit v4 on v3

--- a/solution.py
+++ b/solution.py
@@ -714,8 +714,8 @@
 PLAN = {
     ("start", 0): ((OWN, 0), (OWN, 1), (OWN, 2), (OWN, 3), (OWN, 4),),
     ("qkv", 0): ((RELAY, 0), (RELAY, 1), (HAVE, 0), (HAVE, 1),),
-    ("att", 0): ((RELAY, 2), (RELAY, 3),),
-    ("att1", 0): ((RELAY, 4), (OWN, 5),),
+    ("att", 0): ((RELAY, 2),),
+    ("att1", 0): ((RELAY, 3), (RELAY, 4), (OWN, 5),),
     ("att2", 0): ((DIAG, 2), (DIAG, 3), (OWN, 6),),
     ("mlp", 0): ((DIAG, 4), (HAVE, 2), (HAVE, 3), (HAVE, 4),),
     ("mlp1", 0): ((RELAY, 5), (OWN, 7),),
@@ -739,11 +739,11 @@
     ("b0t1", 0): ((S3, 11),),
     ("b0t2", 0): ((S2, 0), (S3, 8),),
     ("b0t3", 0): ((S4, 3), (S3, 9),),
-    ("b0", 0): ((S3, 10), (V3, 1), (S4, 11),),
-    ("dU", 0): ((S1, 1), (S4, 8),),
+    ("b0", 0): ((S3, 10), (S4, 11),),
+    ("dU", 0): ((S1, 1), (V3, 1), (S4, 8),),
     ("dO", 0): ((S1, 7), (S4, 9), (S2, 1), (S3, 0),),
-    ("pair0", 0): ((S2, 7), (S1, 4), (S4, 10), (V4, 1),),
-    ("pair1", 0): ((S2, 4), (S1, 5),),
+    ("pair0", 0): ((S2, 7), (S1, 4), (S4, 10),),
+    ("pair1", 0): ((S2, 4), (S1, 5), (V4, 1),),
     ("pair2", 0): ((S3, 1), (S2, 5), (S1, 6), (S4, 0),),
     ("half", 0): ((S3, 7), (S2, 6),),
     ("b1", 0): ((V1, 0), (S3, 4),),

time: 122 us -> 120 us (0.984)
  Pallas kernels: 121 us -> 119 us
    pallas_call x1, Pallas kernels: 118 us -> 115 us  [fused(): pl.pallas_call(functools.partial(fused_kernel, names), out_shape=(s((rows...]
where the time goes in v4:
time: 120 us
  Pallas kernels  119 us (99%)
    pallas_call x1, Pallas kernels, fused(): pl.pallas_call(functools.partial(fused_kernel, names), out_shape=(s((rows...  115 us
    pallas_call x1, Pallas kernels, finish(): pl.pallas_call(finish_kernel, out_shape=[jax.ShapeDtypeStruct(t, F32) for...  3.65 us

profile of v4, /device:TPU:0, one launch (start us, length us, event | category | flops | bytes accessed | tf_op | source)
XLA Modules:
  0.0 120.0 jit_solution(7382632880304144217)
XLA Ops:
  0.7 115.5 %shard_map.271 = (f32[1024,384]{1,0:T(8,128)}, f32[1024,384]{1,0:T(8,128)}, bf16[6,4,48,384]{3,2,1,0:T(8,128)(2,1)}, f32[2,12,384]{2,1,0:T(8,128)}) custom-call(f32[1024,384]{1,0:T(8,128)} %refs_0_.1, f32[1024,384]{1,0:T(8,128)} %refs_1_.1, s32[1,1024]{1,0:T(1,128)} %bitcast.1, bf16[2,48]{1,0:T(2,128)(2,1)} %refs_3_.1, bf16[2,48]{1,0:T(2,128)(2,1)} %refs_4_.1, ...), custom_call_target="tpu_custom_call" | custom-call | tf_op jit(solution)/shard_map/pallas_call | solution.py:795
  116.1 3.6 %shard_map.272 = (f32[1024,384]{1,0:T(8,128)}, f32[1024,384]{1,0:T(8,128)}, f32[2,48]{1,0:T(2,128)}, f32[2,48]{1,0:T(2,128)}, f32[2,48,1152]{2,1,0:T(8,128)}, /*...) custom-call(f32[1024,384]{1,0:T(8,128)} %get-tuple-element.19.refs_0, ...), custom_call_target="tpu_custom_call" | custom-call | tf_op jit(solution)/shard_map/pallas_call | solution.py:855
